TPU v7x, 32 devices: a whole 2x2x4 slice. The times are simulated.
32 devices in a mesh: dp: 8 (over y, x, core), mp: 4 (over z).
Axes of the slice: x: 2, y: 2, z: 4, core: 2. Of those that a mesh axis runs over, the one named last changes fastest.
Arguments:
- block_input: bfloat16 [192, 196, 512], P('dp'), may hold values from -6 to 6
- out_grad: bfloat16 [192, 196, 512], P('dp'), may hold values from -6 to 6
- norm_gains: bfloat16 [512, 2], P('dp'), may hold values from 0.5 to 1.5
- offsets: bfloat16 [512, 4], P('dp'), may hold values from -3 to 3
- qkv_weight: bfloat16 [512, 3, 512], P('dp', None, 'mp'), may hold values from -2 to 2
- qv_bias: bfloat16 [2, 512], P(None, 'mp'), may hold values from -3 to 3
- pos_table: float32 [16, 169], P('mp'), may hold values from -4 to 4
- proj_weight: bfloat16 [512, 512], P('dp', 'mp'), may hold values from -0.75 to 0.75
- fc1_weight: bfloat16 [512, 2048], P('dp', 'mp'), may hold values from -0.25 to 0.25
- fc1_bias: bfloat16 [2048], P('mp'), may hold values from -3 to 3
- fc2_weight: bfloat16 [512, 2048], P('dp', 'mp'), may hold values from -0.125 to 0.125
- rel_index: int32 [49, 49], replicated, may hold values from 0 to 168
- region_ids: int32 [14, 14], replicated, may hold values from 0 to 3
Outputs:
- block_output: bfloat16 [192, 196, 512], P('dp')
- input_grad: bfloat16 [192, 196, 512], P('dp')
- norm_gains_grad: float32 [512, 2], P('dp')
- offsets_grad: float32 [512, 4], P('dp')
- qkv_weight_grad: float32 [512, 3, 512], P('dp', None, 'mp')
- qv_bias_grad: float32 [2, 512], P(None, 'mp')
- pos_table_grad: float32 [16, 169], P('mp')
- proj_weight_grad: float32 [512, 512], P('dp', 'mp')
- fc1_weight_grad: float32 [512, 2048], P('dp', 'mp')
- fc1_bias_grad: float32 [2048], P('mp')
- fc2_weight_grad: float32 [512, 2048], P('dp', 'mp')
All inputs are finite; a program needn't handle non-finite values.
Results may differ from a plain program's by a relative error of at most 0.04.
The roundings to bfloat16 on the way count: a program that leaves them out, or rounds other values in their place, can miss the bound.
Values may be sent and summed in bfloat16 or wider, within the bound.
A program may use at most 256 MiB of HBM per device.

v0:
```python
import math

import jax
import jax.numpy as jnp
from jax import lax
from jax.sharding import PartitionSpec as P

D = 512
HD = 32
WIN = 7
SHIFT = 3
SIDE = 14
TOK_IMG = 196


def window_order(tokens_in):
    image_count, channels = (tokens_in.shape[0], tokens_in.shape[-1])
    side_wins = SIDE // WIN
    grid_view = jnp.roll(
        tokens_in.reshape(image_count, SIDE, SIDE, channels), (-SHIFT, -SHIFT), axis=(1, 2)
    )
    grid_view = grid_view.reshape(image_count, side_wins, WIN, side_wins, WIN, channels).transpose(
        0, 1, 3, 2, 4, 5
    )
    return grid_view.reshape(image_count, SIDE * SIDE, channels)


def grid_order(tokens_in):
    image_count, channels = (tokens_in.shape[0], tokens_in.shape[-1])
    side_wins = SIDE // WIN
    grid_view = tokens_in.reshape(image_count, side_wins, side_wins, WIN, WIN, channels).transpose(
        0, 1, 3, 2, 4, 5
    )
    grid_view = jnp.roll(
        grid_view.reshape(image_count, SIDE, SIDE, channels), (SHIFT, SHIFT), axis=(1, 2)
    )
    return grid_view.reshape(image_count, SIDE * SIDE, channels)


def layer_norm(values, gain_col, shift_col):
    row_mean = jnp.mean(values, axis=-1, keepdims=True)
    centred = values - row_mean
    variance = jnp.mean(centred * centred, axis=-1, keepdims=True)
    inv_std = lax.rsqrt(variance + 1e-05)
    normed = centred * inv_std
    return (normed, inv_std, normed * gain_col + shift_col)


def norm_back(grad_out, normed, inv_std, gain_col):
    scaled = grad_out * gain_col
    return inv_std * (
        scaled
        - jnp.mean(scaled, axis=-1, keepdims=True)
        - normed * jnp.mean(scaled * normed, axis=-1, keepdims=True)
    )


def gelu_parts(pre_act):
    cdf_val = 0.5 * (1.0 + jax.scipy.special.erf(pre_act * (1.0 / math.sqrt(2.0))))
    density = jnp.exp(-0.5 * pre_act * pre_act) * (1.0 / math.sqrt(2.0 * math.pi))
    return (pre_act * cdf_val, cdf_val + pre_act * density)


def window_terms(table_rows, rel_index, region_ids, block_size):
    table_len = table_rows.shape[1]
    win_pos = rel_index.shape[0]
    one_hot = (
        rel_index.reshape(-1)[:, None] == jnp.arange(table_len, dtype=jnp.int32)[None, :]
    ).astype(jnp.float32)
    pos_bias = jnp.dot(table_rows, one_hot.T, precision=lax.Precision.HIGHEST).reshape(
        -1, win_pos, win_pos
    )
    side_wins = SIDE // WIN
    labels = (
        region_ids.reshape(side_wins, WIN, side_wins, WIN)
        .transpose(0, 2, 1, 3)
        .reshape(side_wins * side_wins, win_pos)
    )
    penalty = jnp.where(labels[:, :, None] == labels[:, None, :], 0.0, -100.0).astype(jnp.float32)
    win_bias = pos_bias[None] + penalty[:, None]
    return (jnp.tile(win_bias, (block_size, 1, 1, 1)), one_hot)


def blocked():
    for block_size in range(12, 0, -1):
        return block_size
    return 1


def along_rows(left_mat, right_mat):
    return lax.dot_general(
        left_mat, right_mat, (((0,), (0,)), ((), ())), preferred_element_type=jnp.float32
    )


def along_cols(left_mat, right_mat):
    return lax.dot_general(
        left_mat, right_mat, (((1,), (1,)), ((), ())), preferred_element_type=jnp.float32
    )


def attend(queries, key_rows, values, win_bias):
    scores = (
        jnp.einsum("bqhc,bkhc->bhqk", queries, key_rows, preferred_element_type=jnp.float32)
        + win_bias
    )
    row_max = jnp.max(scores, axis=-1, keepdims=True)
    weights_raw = jnp.exp(scores - row_max)
    row_total = jnp.sum(weights_raw, axis=-1, keepdims=True)
    probs = (weights_raw / row_total).astype(jnp.bfloat16)
    attn_rows = jnp.einsum(
        "bhqk,bkhc->bqhc", probs, values, preferred_element_type=jnp.float32
    ).astype(jnp.bfloat16)
    return (attn_rows, (row_max + jnp.log(row_total))[..., 0])


def attend_back(queries, key_rows, values, attn_rows, grad_attn, log_total, win_bias, score_scale):
    scores = (
        jnp.einsum("bqhc,bkhc->bhqk", queries, key_rows, preferred_element_type=jnp.float32)
        + win_bias
    )
    probs = jnp.exp(scores - log_total[..., None])
    grad_probs = jnp.einsum(
        "bqhc,bkhc->bhqk", grad_attn, values, preferred_element_type=jnp.float32
    )
    delta = jnp.sum(
        grad_attn.astype(jnp.float32) * attn_rows.astype(jnp.float32), axis=-1
    ).transpose(0, 2, 1)
    grad_scores = probs * (grad_probs - delta[..., None])
    grad_sb = grad_scores.astype(jnp.bfloat16)
    grad_q = (
        jnp.einsum("bhqk,bkhc->bqhc", grad_sb, key_rows, preferred_element_type=jnp.float32)
        * score_scale
    )
    grad_k = jnp.einsum("bhqk,bqhc->bkhc", grad_sb, queries, preferred_element_type=jnp.float32)
    grad_v = jnp.einsum(
        "bhqk,bqhc->bkhc", probs.astype(jnp.bfloat16), grad_attn, preferred_element_type=jnp.float32
    )
    table_part = jnp.sum(grad_scores, axis=0)
    return (grad_q, grad_k, grad_v, table_part)


def fetch_weights(norm_gains, offsets, qkv_weight, proj_weight, fc1_weight, fc2_weight):
    return (
        lax.all_gather(norm_gains, "dp", axis=0, tiled=True),
        lax.all_gather(offsets, "dp", axis=0, tiled=True),
        lax.all_gather(qkv_weight, "dp", axis=0, tiled=True),
        lax.all_gather(proj_weight, "dp", axis=0, tiled=True),
        lax.all_gather(fc1_weight, "dp", axis=0, tiled=True),
        lax.all_gather(fc2_weight, "dp", axis=0, tiled=True),
    )


def shards(
    block_input,
    out_grad,
    norm_gains,
    offsets,
    qkv_weight,
    qv_bias,
    pos_table,
    proj_weight,
    fc1_weight,
    fc1_bias,
    fc2_weight,
    rel_index,
    region_ids,
):
    win_pos = rel_index.shape[0]
    win_count = TOK_IMG // win_pos
    score_scale = HD ** (-0.5)
    image_count = block_input.shape[0]
    row_count = image_count * TOK_IMG
    heads_here = pos_table.shape[0]
    head_cols = heads_here * HD
    block_size = blocked()
    block_count = image_count // block_size
    win_bias, one_hot = window_terms(pos_table, rel_index, region_ids, block_size)

    def split_heads(flat_rows):
        return flat_rows.reshape(block_count, block_size * win_count, win_pos, heads_here, HD)

    def forward_block(operands):
        return attend(operands[0], operands[1], operands[2], win_bias)

    def backward_block(operands):
        return attend_back(
            operands[0],
            operands[1],
            operands[2],
            operands[3],
            operands[4],
            operands[5],
            win_bias,
            score_scale,
        )

    def gather_all():
        fetched = tuple(
            fetch_weights(norm_gains, offsets, qkv_weight, proj_weight, fc1_weight, fc2_weight)
        )
        return fetched + (qv_bias, fc1_bias)

    gains_w, offsets_w, qkv_w, proj_w, fc1_w, fc2_w, pair_bias, hidden_bias = gather_all()
    gain_cols = gains_w.astype(jnp.float32)
    offset_cols = offsets_w.astype(jnp.float32)
    bias_qv = pair_bias.astype(jnp.float32)
    x_zero = window_order(block_input).reshape(row_count, D).astype(jnp.float32)
    normed1, inv_std1, pre_one = layer_norm(x_zero, gain_cols[:, 0], offset_cols[:, 0])
    h_one = pre_one.astype(jnp.bfloat16)
    qkv_all = jnp.dot(
        h_one, qkv_w.reshape(D, 3 * head_cols), preferred_element_type=jnp.float32
    ).reshape(row_count, 3, head_cols)
    queries = ((qkv_all[:, 0] + bias_qv[0]) * score_scale).astype(jnp.bfloat16)
    key_rows = qkv_all[:, 1].astype(jnp.bfloat16)
    values = (qkv_all[:, 2] + bias_qv[1]).astype(jnp.bfloat16)
    attn_rows, log_total = lax.map(
        forward_block, (split_heads(queries), split_heads(key_rows), split_heads(values))
    )
    attn_flat = attn_rows.reshape(row_count, head_cols)
    attn_out = lax.psum(along_cols(attn_flat, proj_w).astype(jnp.bfloat16), "mp").astype(
        jnp.float32
    )
    x_one = x_zero + attn_out + offset_cols[:, 1]
    normed2, inv_std2, pre_two = layer_norm(x_one, gain_cols[:, 1], offset_cols[:, 2])
    h_two = pre_two.astype(jnp.bfloat16)
    pre_act = jnp.dot(h_two, fc1_w, preferred_element_type=jnp.float32) + hidden_bias.astype(
        jnp.float32
    )
    act_val, act_slope = gelu_parts(pre_act)
    act_rows = act_val.astype(jnp.bfloat16)
    mlp_out = lax.psum(along_cols(act_rows, fc2_w).astype(jnp.bfloat16), "mp").astype(jnp.float32)
    block_rows = (x_one + mlp_out + offset_cols[:, 3]).astype(jnp.bfloat16)
    out_images = grid_order(block_rows.reshape(image_count, TOK_IMG, D))
    gains_w, offsets_w, qkv_w, proj_w, fc1_w, fc2_w, pair_bias, hidden_bias = gather_all()
    gain_cols = gains_w.astype(jnp.float32)
    offset_cols = offsets_w.astype(jnp.float32)
    grad_y = window_order(out_grad).reshape(row_count, D)
    grad_yf = grad_y.astype(jnp.float32)
    grad_fc2b = jnp.sum(grad_yf, axis=0)
    grad_fc2 = along_rows(grad_y, act_rows)
    grad_pre = jnp.dot(grad_y, fc2_w, preferred_element_type=jnp.float32) * act_slope
    grad_preb = grad_pre.astype(jnp.bfloat16)
    grad_fc1 = along_rows(h_two, grad_preb)
    grad_fc1b = jnp.sum(grad_pre, axis=0)
    grad_h2 = lax.psum(along_cols(grad_preb, fc1_w).astype(jnp.bfloat16), "mp").astype(jnp.float32)
    grad_ln2 = jnp.sum(grad_h2 * normed2, axis=0)
    grad_ln2b = jnp.sum(grad_h2, axis=0)
    grad_x1 = grad_yf + norm_back(grad_h2, normed2, inv_std2, gain_cols[:, 1])
    grad_x1b = grad_x1.astype(jnp.bfloat16)
    grad_proj = along_rows(grad_x1b, attn_flat)
    grad_projb = jnp.sum(grad_x1, axis=0)
    grad_attn = jnp.dot(grad_x1b, proj_w, preferred_element_type=jnp.float32).astype(jnp.bfloat16)
    grad_q, grad_k, grad_v, table_part = lax.map(
        backward_block,
        (
            split_heads(queries),
            split_heads(key_rows),
            split_heads(values),
            split_heads(attn_flat),
            split_heads(grad_attn),
            log_total,
        ),
    )
    grad_q = grad_q.reshape(row_count, head_cols)
    grad_k = grad_k.reshape(row_count, head_cols)
    grad_v = grad_v.reshape(row_count, head_cols)
    grad_qv = jnp.stack([jnp.sum(grad_q, axis=0), jnp.sum(grad_v, axis=0)])
    grad_qkv = (
        jnp.stack([grad_q, grad_k, grad_v], axis=1)
        .astype(jnp.bfloat16)
        .reshape(row_count, 3 * head_cols)
    )
    grad_qkvw = along_rows(h_one, grad_qkv).reshape(D, 3, head_cols)
    grad_h1 = lax.psum(
        along_cols(grad_qkv, qkv_w.reshape(D, 3 * head_cols)).astype(jnp.bfloat16), "mp"
    ).astype(jnp.float32)
    grad_ln1 = jnp.sum(grad_h1 * normed1, axis=0)
    grad_ln1b = jnp.sum(grad_h1, axis=0)
    grad_x0 = grad_x1 + norm_back(grad_h1, normed1, inv_std1, gain_cols[:, 0])
    input_share = grid_order(grad_x0.astype(jnp.bfloat16).reshape(image_count, TOK_IMG, D))
    table_grad = jnp.dot(
        jnp.sum(table_part, axis=0).reshape(heads_here, -1),
        one_hot,
        precision=lax.Precision.HIGHEST,
    )
    gains_grad = jnp.stack([grad_ln1, grad_ln2], axis=1)
    offsets_grad = jnp.stack([grad_ln1b, grad_projb, grad_ln2b, grad_fc2b], axis=1)
    grad_qv, table_grad, grad_fc1b = lax.psum((grad_qv, table_grad, grad_fc1b), "dp")
    gains_grad, offsets_grad, grad_qkvw, grad_proj, grad_fc1, grad_fc2 = (
        lax.psum_scatter(
            gains_grad.astype(jnp.bfloat16), "dp", scatter_dimension=0, tiled=True
        ).astype(jnp.float32),
        lax.psum_scatter(
            offsets_grad.astype(jnp.bfloat16), "dp", scatter_dimension=0, tiled=True
        ).astype(jnp.float32),
        lax.psum_scatter(
            grad_qkvw.astype(jnp.bfloat16), "dp", scatter_dimension=0, tiled=True
        ).astype(jnp.float32),
        lax.psum_scatter(
            grad_proj.astype(jnp.bfloat16), "dp", scatter_dimension=0, tiled=True
        ).astype(jnp.float32),
        lax.psum_scatter(
            grad_fc1.astype(jnp.bfloat16), "dp", scatter_dimension=0, tiled=True
        ).astype(jnp.float32),
        lax.psum_scatter(
            grad_fc2.astype(jnp.bfloat16), "dp", scatter_dimension=0, tiled=True
        ).astype(jnp.float32),
    )
    return (
        out_images,
        input_share,
        gains_grad,
        offsets_grad,
        grad_qkvw,
        grad_qv,
        table_grad,
        grad_proj,
        grad_fc1,
        grad_fc1b,
        grad_fc2,
    )


def solution(mesh):
    in_specs = (
        P("dp", None, None),
        P("dp", None, None),
        P("dp", None),
        P("dp", None),
        P("dp", None, "mp"),
        P(None, "mp"),
        P("mp", None),
        P("dp", "mp"),
        P("dp", "mp"),
        P("mp"),
        P("dp", "mp"),
        P(),
        P(),
    )
    out_specs = (
        P("dp", None, None),
        P("dp", None, None),
        P("dp", None),
        P("dp", None),
        P("dp", None, "mp"),
        P(None, "mp"),
        P("mp", None),
        P("dp", "mp"),
        P("dp", "mp"),
        P("mp"),
        P("dp", "mp"),
    )
    return jax.shard_map(shards, mesh=mesh, in_specs=in_specs, out_specs=out_specs, check_vma=False)
```

profile of v0, /device:TPU:0, one launch (start us, length us, event | category | flops | bytes accessed | tf_op | source)
XLA Modules:
  0.0 1214.7 jit_solution(2443523745431153764)
XLA Ops:
  12.8 10.3 all-gather
  23.2 8.9 all-gather.1
  32.8 8.6 all_gather.25
  54.4 8.4 reshape.269
  72.2 9.4 all_gather.26
  95.5 8.4 copy.112
  103.9 10.7 squeeze.33
  120.9 10.7 squeeze.34
  137.9 21.8 %while.30 = (s32[]{:T(128)}, bf16[2,48,49,4,32]{2,4,3,1,0:T(8,128)(2,1)}, f32[2,48,4,49]{3,2,1,0:T(4,128)S(1)}, bf16[2,48,49,4,32]{2,4,3,1,0:T(8,128)(2,1)}, bf1...) while((s32[]{:T(128)}, ...), condition=%wide.region_5.6_spmd.clone, body=%wide.region_2.5_spmd.clone.sunk | while | flops 63447552 | bytes 31814608 | solution.py:217
  187.7 8.4 reshape_reshape.11
  199.9 9.7 copy.101
  209.5 11.5 reshape.259
  221.1 9.9 all_gather.27
  231.0 11.2 all_gather.28
  242.2 109.5 %all-reduce.6.cloned.1.call-done = bf16[4704,512]{1,0:T(8,128)(2,1)} async-done(((bf16[4704,512]{1,0:T(8,128)(2,1)}), bf16[4704,512]{1,0:T(8,128)(2,1)}) %all-reduce.6.cloned.1.call-update) | async-done | bytes 4816912 | tf_op jit(solution)/shard_map/psum | solution.py:221
  351.6 10.0 fusion.98
  377.5 9.0 fusion.103
  408.3 159.2 %all-reduce.8.cloned.1.call-done = bf16[4704,512]{1,0:T(8,128)(2,1)} async-done(((bf16[4704,512]{1,0:T(8,128)(2,1)}), bf16[4704,512]{1,0:T(8,128)(2,1)}) %all-reduce.8.cloned.1.call-update) | async-done | bytes 4816912 | tf_op jit(solution)/shard_map/psum | solution.py:246
  567.5 10.3 fusion.53
  598.9 8.7 copy.121
  607.6 42.0 %while.31 = (s32[]{:T(128)}, f32[2,48,49,4,32]{2,4,3,1,0:T(8,128)}, bf16[2,48,49,4,32]{2,4,3,1,0:T(8,128)(2,1)}, f32[2,48,49,4,32]{2,4,3,1,0:T(8,128)}, f32[2,4,...) while((s32[]{:T(128)}, f32[2,48,49,4,32]{2,4,3,1,0:T(8,128)}, ...), condition=%wide.region_16.17_spmd.clone, body=%wide.region_13.16_spmd.clone.sunk | while | flops 153152640 | bytes 111455464 | solution.py:254
  649.7 10.1 copy.137
  666.3 10.1 copy.139
  738.0 14.6 %all-reduce = (f32[2,128]{1,0:T(2,128)}, f32[4,169]{1,0:T(4,128)}, f32[512]{0:T(512)}) all-reduce(f32[2,128]{1,0:T(2,128)S(1)} %pad_maximum_fusion.9, f32[4,169]{1,0:T(4,128)S(1)} %fusion.73, f32[512]{0:T(512)S(1)} %copy-done.48), channel_id=1, replica_groups=mesh['dp'=8,'mp'=4] {'dp'}, use_global_device_ids=true, to_apply=%region_31.32 | all-reduce | flops 1444 | bytes 11552 | tf_op jit(solution)/shard_map/psum | solution.py:289
  754.0 18.8 %reduce-scatter.11.cloned.1.call-done = bf16[64,3,128]{2,0,1:T(8,128)(2,1)} async-done(((bf16[512,3,128]{2,0,1:T(8,128)(2,1)}), bf16[64,3,128]{2,0,1:T(8,128)(2,1)}) %reduce-scatter.11.cloned.1.call-update) | async-done | bytes 49168 | tf_op jit(solution)/shard_map/reduce_scatter | solution.py:297
  774.3 332.8 %all-reduce.10.cloned.1.call-done = (bf16[4704,512]{1,0:T(8,128)(2,1)}, bf16[4704,512]{1,0:T(8,128)(2,1)}) async-done(((bf16[4704,512]{1,0:T(8,128)(2,1)}, bf16[4704,512]{1,0:T(8,128)(2,1)}), (bf16[4704,512]{1,0:T(8,128)(2,1)}, bf16[4704,512]{1,0:T(8,128)(2,1)})) %all-reduce.10.cloned.1.call-update) | async-done | bytes 9633808 | tf_op jit(solution)/shard_map/psum | solution.py:232
  1110.1 10.3 fusion.59
  1121.4 9.2 add_convert_fusion
  1130.6 10.3 fusion.57
  1140.9 8.3 reshape_reshape.10
  1157.0 8.3 reshape_reshape.12
  1183.6 23.0 %reduce-scatter.21.cloned.1.call-done = bf16[64,4]{1,0:T(8,128)(2,1)} async-done(((bf16[512,4]{1,0:T(8,128)(2,1)}), bf16[64,4]{1,0:T(8,128)(2,1)}) %reduce-scatter.21.cloned.1.call-update) | async-done | bytes 528
  (330 shorter events, 310.5 us)
Async XLA Ops:
  7.2 63.6 %copy-start = (f32[4,169]{1,0:T(4,128)S(1)}, f32[4,169]{1,0:T(4,128)}, u32[]{:S(2)}) copy-start(f32[4,169]{1,0:T(4,128)} %param.23) | copy-start | bytes 8116
  7.2 344.4 %all-reduce.6.cloned.1.call-start = ((), (), s32[]{:S(2)}) async-start(), calls=%async_computation.6 | async-start | bytes 9633792 | tf_op jit(solution)/shard_map/psum | solution.py:221
  7.3 15.9 %copy-start.49 = (bf16[64,4]{0,1:T(4,128)(2,1)S(1)}, bf16[64,4]{0,1:T(4,128)(2,1)}, u32[]{:S(2)}) copy-start(bf16[64,4]{0,1:T(4,128)(2,1)} %param.20) | copy-start | bytes 1540
  7.3 25.5 %copy-start.37 = (bf16[64,3,128]{2,0,1:T(8,128)(2,1)S(1)}, bf16[64,3,128]{2,0,1:T(8,128)(2,1)}, u32[]{:S(2)}) copy-start(bf16[64,3,128]{2,0,1:T(8,128)(2,1)} %param.21) | copy-start | bytes 147460
  23.2 24.7 %copy-start.38 = (f32[512,1]{0,1:T(1,128)}, f32[512,1]{0,1:T(1,128)S(1)}, u32[]{:S(2)}) copy-start(f32[512,1]{0,1:T(1,128)S(1)} %get-tuple-element.312) | copy-start | bytes 6148
  70.5 17.7 %copy-start.42 = (s32[2401]{0:T(1024)}, s32[2401]{0:T(1024)S(1)}, u32[]{:S(2)}) copy-start(s32[2401]{0:T(1024)S(1)} %eq.34) | copy-start | bytes 28816
  176.1 391.4 %all-reduce.8.cloned.1.call-start = ((), (), s32[]{:S(2)}) async-start(), calls=%async_computation.7 | async-start | bytes 9633792 | tf_op jit(solution)/shard_map/psum | solution.py:246
  209.5 11.5 copy-start.36
  368.1 9.3 slice-start.6
  393.3 330.4 %reduce-scatter.15.cloned.1.call-start = ((), (), s32[]{:S(2)}) async-start(), calls=%async_computation.10 | async-start | bytes 589824 | tf_op jit(solution)/shard_map/reduce_scatter | solution.py:303
  400.8 324.4 %reduce-scatter.17.cloned.1.call-start = ((), (), s32[]{:S(2)}) async-start(), calls=%async_computation.11 | async-start | bytes 589824 | tf_op jit(solution)/shard_map/reduce_scatter | solution.py:306
  408.2 344.4 %reduce-scatter.13.cloned.1.call-start = ((), (), s32[]{:S(2)}) async-start(), calls=%async_computation.9 | async-start | bytes 147456 | tf_op jit(solution)/shard_map/reduce_scatter | solution.py:300
  615.1 6.8 slice-start.4
  615.2 6.8 slice-start.5
  615.2 8.3 slice-start.2
  636.1 6.8 slice-start.4
  636.2 8.3 slice-start.2
  690.5 6.9 copy-start.17
  703.4 69.4 %reduce-scatter.11.cloned.1.call-start = ((), (), s32[]{:S(2)}) async-start(), calls=%async_computation.8 | async-start | bytes 442368 | tf_op jit(solution)/shard_map/reduce_scatter | solution.py:297
  710.0 7.0 copy-start.24
  710.1 397.0 %all-reduce.10.cloned.1.call-start = ((), (), s32[]{:S(2)}) async-start(), calls=%async_computation.14 | async-start | bytes 19267584 | tf_op jit(solution)/shard_map/psum | solution.py:232
  710.1 6.9 copy-start.26
  710.1 6.9 copy-start.27
  721.4 460.8 %reduce-scatter.19.cloned.1.call-start = ((), (), s32[]{:S(2)}) async-start(), calls=%async_computation.12 | async-start | bytes 147456
  730.1 7.0 copy-start.43
  730.1 7.9 copy-start.48
  733.7 376.4 %copy-start.39 = (f32[512,1]{0,1:T(1,128)S(1)}, f32[512,1]{0,1:T(1,128)}, u32[]{:S(2)}) copy-start(f32[512,1]{0,1:T(1,128)} %copy-done.38) | copy-start | bytes 6148
  1110.1 11.3 copy-start.44
  1110.1 20.5 %slice-start = ((s8[4816896]{0:T(1024)(128)(4,1)}), s8[622592]{0:T(1024)(128)(4,1)S(1)}, s32[]{:S(2)}) async-start(s8[4816896]{0:T(1024)(128)(4,1)} %bitcast.240), calls=%async_computation.15 | async-start | bytes 1245184
  1121.3 85.3 %reduce-scatter.21.cloned.1.call-start = ((), (), s32[]{:S(2)}) async-start(), calls=%async_computation.13 | async-start | bytes 147456
  1121.4 9.2 slice-start.1
  1173.9 34.1 %copy-start.1 = (f32[4,169]{1,0:T(4,128)S(1)}, f32[4,169]{1,0:T(4,128)}, u32[]{:S(2)}) copy-start(f32[4,169]{1,0:T(4,128)} %param.23) | copy-start | bytes 8116
  (55 other events, 210.1 us)
Sparse Core Ops, SparseCore 0:
  176.2 175.3 all-reduce.5
  393.4 174.0 all-reduce.7
  570.6 33.0 reduce-scatter.14
  606.6 34.1 reduce-scatter.16
  703.5 32.4 reduce-scatter.12
  738.9 33.8 reduce-scatter.10
  776.0 330.9 all-reduce.9
  1121.4 32.5 reduce-scatter.18
  1174.0 32.5 reduce-scatter.20
where the time goes:
time: 1230 us; the launch traced here: 1210 us
  waiting for transfers between devices  643 us (52%)
  local copies, waits for them, and re-layouts  245 us (20%)
  other arithmetic  128 us (10%)
  matrix products  109 us (9%)
  blocking collectives  72.9 us (6%)
  between operations  14.8 us (1%)
    psum x1, waiting for transfers between devices, shards(): lax.psum(along_cols(act_rows, fc2_w).astype(jnp.bfloat16), 'mp')  333 us
    psum x1, waiting for transfers between devices, shards(): lax.psum(along_cols(grad_preb, fc1_w).astype(jnp.bfloat16), 'mp')  159 us
    psum x1, waiting for transfers between devices, shards(): lax.psum(along_cols(attn_flat, proj_w).astype(jnp.bfloat16), 'mp')  109 us
    another operation x6, local copies, waits for them, and re-layouts, shards(): jnp.stack([grad_q, grad_k, grad_v], axis=1).astype(jnp.bfloat16)  47.7 us
    unnamed x101, local copies, waits for them, and re-layouts  35.7 us
    dot_general x4, matrix products, along_rows(): lax.dot_general(left_mat, right_mat, (((0,), (0,)), ((), ())), preferred_...  27.4 us
  transfers between devices with their start and end apart: 9, of which 5 were waited for; matrix products, arithmetic and copies ran while one was open for 23% of the time, Pallas kernels for 0%

commit v1 on v0

v1 whole, which is shorter than its diff:
```python
import functools
import math

import jax
import jax.numpy as jnp
import numpy as np
from jax import lax
from jax.experimental import pallas as pl
from jax.experimental.pallas import tpu as pltpu
from jax.sharding import PartitionSpec as P

HD = 32
WIN = 7
SHIFT = 3
SIDE = 14
F32 = jnp.float32
BF16 = jnp.bfloat16
WPAD = 64
EPS = 1e-05
DEAD = -1e30


def dot(a, b, ca=1, cb=0):
    return lax.dot_general(a, b, (((ca,), (cb,)), ((), ())), preferred_element_type=F32)


def padded_order():
    sides = SIDE // WIN
    wpos = WIN * WIN
    rows = np.full((sides * sides * WPAD,), -1, np.int32)
    for wr in range(sides):
        for wc in range(sides):
            for a in range(wpos):
                r = (wr * WIN + a // WIN + SHIFT) % SIDE
                c = (wc * WIN + a % WIN + SHIFT) % SIDE
                rows[(wr * sides + wc) * WPAD + a] = r * SIDE + c
    return rows


def pick_matrix(tokens):
    rows = padded_order()
    return (rows[:, None] == np.arange(tokens)[None, :]).astype(np.float32)


def norm(x):
    mean = jnp.mean(x, axis=-1, keepdims=True)
    cen = x - mean
    var = jnp.mean(cen * cen, axis=-1, keepdims=True)
    inv = lax.rsqrt(var + EPS)
    return cen * inv, inv


def norm_back(grad, normed, inv, gain):
    scaled = grad * gain
    return inv * (
        scaled
        - jnp.mean(scaled, axis=-1, keepdims=True)
        - normed * jnp.mean(scaled * normed, axis=-1, keepdims=True)
    )


def col_sum(v):
    return jnp.sum(v, axis=0, keepdims=True)


def head_masks(group_heads):
    lane_q = lax.broadcasted_iota(jnp.int32, (group_heads * WPAD, group_heads * HD), 0)
    lane_c = lax.broadcasted_iota(jnp.int32, (group_heads * WPAD, group_heads * HD), 1)
    return (lane_q // WPAD) == (lane_c // HD)


def spread(rows, mask, group_heads):
    tiled = jnp.concatenate([rows] * group_heads, axis=0)
    return jnp.where(mask, tiled, jnp.zeros_like(tiled))


def gather_heads(full, mask, group_heads):
    kept = jnp.where(mask, full, 0.0)
    total = kept[0:WPAD]
    for h in range(1, group_heads):
        total = total + kept[h * WPAD : (h + 1) * WPAD]
    return total


def attention_kernel(
    off_ref, x_ref, w_ref, vec_ref, qvb_ref, bias_ref, pm_ref, pmt_ref,
    qkv_ref, hw_ref, probs_ref, attn_ref, attw, *, imgs, groups, gh, prow, trow,
):
    gc = gh * HD
    full = groups * gc
    gain = vec_ref[0:1, :]
    shift = vec_ref[2:3, :]
    for im in range(imgs):
        normed, _ = norm(x_ref[im].astype(F32))
        h1 = (normed * gain + shift).astype(BF16)
        hw_ref[im * prow : (im + 1) * prow, :] = dot(pm_ref[...], h1).astype(BF16)
    hw = hw_ref[...]
    for kind in range(3):
        wk = jnp.concatenate([w_ref[g, :, kind * gc : (kind + 1) * gc] for g in range(groups)], axis=1)
        part = dot(hw, wk)
        if kind == 0:
            part = (part + qvb_ref[0:1, :]) * (HD**-0.5)
        if kind == 2:
            part = part + qvb_ref[1:2, :]
        qkv_ref[:, kind * full : (kind + 1) * full] = part.astype(BF16)
    wins = prow // WPAD
    mask = head_masks(gh)

    def window(i, carry):
        rows = pl.ds(pl.multiple_of(i * WPAD, WPAD), WPAD)
        win = lax.rem(i, wins)
        for g in range(groups):
            q = qkv_ref[rows, g * gc : (g + 1) * gc]
            k = qkv_ref[rows, full + g * gc : full + (g + 1) * gc]
            v = qkv_ref[rows, 2 * full + g * gc : 2 * full + (g + 1) * gc]
            scores = dot(k, spread(q, mask, gh), 1, 1) + bias_ref[g, win]
            e = jnp.exp(scores - jnp.max(scores, axis=0, keepdims=True))
            p = e * (1.0 / jnp.sum(e, axis=0, keepdims=True))
            probs_ref[i, g] = p
            o = gather_heads(dot(p.astype(BF16), v, 0, 0), mask, gh)
            attw[rows, g * gc : (g + 1) * gc] = o.astype(BF16)
        return carry

    lax.fori_loop(0, imgs * wins, window, 0)
    for im in range(imgs):
        attn_ref[im * trow : (im + 1) * trow, :] = dot(
            pmt_ref[...], attw[im * prow : (im + 1) * prow, :]
        ).astype(BF16)


def gelu_parts(pre):
    cdf = 0.5 * (1.0 + lax.erf(pre * (1.0 / math.sqrt(2.0))))
    density = jnp.exp(-0.5 * pre * pre) * (1.0 / math.sqrt(2.0 * math.pi))
    return pre * cdf, cdf + pre * density


def feed_kernel(
    off_ref, x_ref, gy_ref, attn_ref, w_ref, vec_ref, hb_ref,
    out_ref, gx1_ref, gw_ref, gb_ref, sums_ref,
    xs, gys, h2s, gyt, h2t, mlp, gh2, acc_p, acc_1, acc_2, *, imgs, groups, gc, trow, tokens,
):
    step = pl.program_id(0)
    d = vec_ref.shape[1]
    hid = hb_ref.shape[2]

    @pl.when(step == 0)
    def _():
        acc_p[...] = jnp.zeros_like(acc_p)
        acc_1[...] = jnp.zeros_like(acc_1)
        acc_2[...] = jnp.zeros_like(acc_2)
        gb_ref[...] = jnp.zeros_like(gb_ref)
        sums_ref[...] = jnp.zeros_like(sums_ref)
        xs[...] = jnp.zeros_like(xs)
        gys[...] = jnp.zeros_like(gys)

    for im in range(imgs):
        xs[im * trow : im * trow + tokens, :] = x_ref[im].astype(F32)
        gys[im * trow : im * trow + tokens, :] = gy_ref[im].astype(F32)
    proj = jnp.concatenate([w_ref[g, :, 0:gc] for g in range(groups)], axis=1)
    attn = attn_ref[...]
    x1 = xs[...] + dot(attn, proj, 1, 1) + vec_ref[3:4, :]
    xs[...] = x1
    normed2, inv2 = norm(x1)
    h2f = normed2 * vec_ref[1:2, :] + vec_ref[4:5, :]
    h2s[...] = h2f.astype(BF16)
    h2t[...] = h2f.T.astype(BF16)
    gyt[...] = gys[...].T.astype(BF16)
    mlp[...] = jnp.zeros_like(mlp)
    gh2[...] = jnp.zeros_like(gh2)

    def group(g, carry):
        fc1 = w_ref[g, :, gc : gc + hid]
        fc2 = w_ref[g, :, gc + hid : gc + 2 * hid]
        pre = dot(h2s[...], fc1) + hb_ref[g]
        act, slope = gelu_parts(pre)
        act = act.astype(BF16)
        gpre = dot(gys[...].astype(BF16), fc2) * slope
        gpb = gpre.astype(BF16)
        gb_ref[g] += col_sum(gpre)
        mlp[...] += dot(act, fc2, 1, 1)
        acc_2[g] += dot(gyt[...], act)
        gh2[...] += dot(gpb, fc1, 1, 1)
        acc_1[g] += dot(h2t[...], gpb)
        return carry

    lax.fori_loop(0, groups, group, 0)
    out = xs[...] + mlp[...] + vec_ref[5:6, :]
    for im in range(imgs):
        out_ref[im] = out[im * trow : im * trow + tokens].astype(BF16)
    normed2, inv2 = norm(xs[...])
    grad = gh2[...]
    gy = gys[...]
    gx1 = gy + norm_back(grad, normed2, inv2, vec_ref[1:2, :])
    gx1_ref[...] = gx1
    gx1b = gx1.astype(BF16)
    acc_p[...] += dot(gx1.T.astype(BF16), attn)
    sums_ref[0:1, :] += col_sum(grad * normed2)
    sums_ref[1:2, :] += col_sum(gx1)
    sums_ref[2:3, :] += col_sum(grad)
    sums_ref[3:4, :] += col_sum(gy)

    @pl.when(step == pl.num_programs(0) - 1)
    def _():
        for g in range(groups):
            gw_ref[g, :, 0:gc] = acc_p[:, g * gc : (g + 1) * gc].astype(BF16)
            gw_ref[g, :, gc : gc + hid] = acc_1[g].astype(BF16)
            gw_ref[g, :, gc + hid : gc + 2 * hid] = acc_2[g].astype(BF16)


def attention_back_kernel(
    off_ref, x_ref, gx1_ref, qkv_ref, hw_ref, probs_ref, wa_ref, wp_ref, vec_ref, pm_ref, pmt_ref,
    gin_ref, gw_ref, table_ref, qvs_ref, sums_ref,
    gxw, ga, gqkv, hwt, acc, *, imgs, groups, gh, prow, trow, tokens,
):
    step = pl.program_id(0)
    gc = gh * HD
    full = groups * gc

    @pl.when(step == 0)
    def _():
        acc[...] = jnp.zeros_like(acc)
        table_ref[...] = jnp.zeros_like(table_ref)
        qvs_ref[...] = jnp.zeros_like(qvs_ref)
        sums_ref[...] = jnp.zeros_like(sums_ref)

    for im in range(imgs):
        gxw[im * prow : (im + 1) * prow, :] = dot(
            pm_ref[...], gx1_ref[im * trow : (im + 1) * trow, :].astype(BF16)
        ).astype(BF16)
    proj = jnp.concatenate([wp_ref[g, :, 0:gc] for g in range(groups)], axis=1)
    ga[...] = dot(gxw[...], proj).astype(BF16)
    hwt[...] = hw_ref[...].astype(F32).T.astype(BF16)
    mask = head_masks(gh)
    wins = prow // WPAD

    def window(i, carry):
        rows = pl.ds(pl.multiple_of(i * WPAD, WPAD), WPAD)
        for g in range(groups):
            cols = slice(g * gc, (g + 1) * gc)
            q = qkv_ref[rows, g * gc : (g + 1) * gc]
            k = qkv_ref[rows, full + g * gc : full + (g + 1) * gc]
            v = qkv_ref[rows, 2 * full + g * gc : 2 * full + (g + 1) * gc]
            p = probs_ref[i, g]
            gas = spread(ga[rows, cols], mask, gh)
            dp = dot(v, gas, 1, 1)
            ds = p * (dp - jnp.sum(p * dp, axis=0, keepdims=True))
            table_ref[g] += ds
            dsb = ds.astype(BF16)
            gq = gather_heads(dot(dsb, k, 0, 0), mask, gh) * (HD**-0.5)
            gk = dot(dsb, spread(q, mask, gh))
            gv = dot(p.astype(BF16), gas)
            qvs_ref[0:1, cols] += col_sum(gq)
            qvs_ref[1:2, cols] += col_sum(gv)
            gqkv[rows, g * gc : (g + 1) * gc] = gq.astype(BF16)
            gqkv[rows, full + g * gc : full + (g + 1) * gc] = gk.astype(BF16)
            gqkv[rows, 2 * full + g * gc : 2 * full + (g + 1) * gc] = gv.astype(BF16)
        return carry

    lax.fori_loop(0, imgs * wins, window, 0)
    gh1 = None
    for kind in range(3):
        wk = jnp.concatenate([wa_ref[g, :, kind * gc : (kind + 1) * gc] for g in range(groups)], axis=1)
        part = gqkv[:, kind * full : (kind + 1) * full]
        term = dot(part, wk, 1, 1)
        gh1 = term if gh1 is None else gh1 + term
        acc[kind] += dot(hwt[...], part)
    gh1b = gh1.astype(BF16)
    for im in range(imgs):
        grad = dot(pmt_ref[...], gh1b[im * prow : (im + 1) * prow])[0:tokens]
        normed, inv = norm(x_ref[im].astype(F32))
        sums_ref[0:1, :] += col_sum(grad * normed)
        sums_ref[1:2, :] += col_sum(grad)
        gx0 = gx1_ref[im * trow : im * trow + tokens, :] + norm_back(grad, normed, inv, vec_ref[0:1, :])
        gin_ref[im] = gx0.astype(BF16)

    @pl.when(step == pl.num_programs(0) - 1)
    def _():
        for g in range(groups):
            for kind in range(3):
                gw_ref[g, :, kind * gc : (kind + 1) * gc] = acc[kind, :, g * gc : (g + 1) * gc].astype(BF16)


def whole(shape):
    zero = (0,) * len(shape)
    return pl.BlockSpec(shape, lambda i, off: zero, pipeline_mode=pl.Buffered(1))


def split3(v):
    hi = lax.reduce_precision(v, 8, 7)
    mid = lax.reduce_precision(v - hi, 8, 7)
    lo = v - hi - mid
    return [hi, mid, lo]


def shards(
    block_input, out_grad, norm_gains, offsets, qkv_weight, qv_bias, pos_table,
    proj_weight, fc1_weight, fc1_bias, fc2_weight, rel_index, region_ids, *, n_dp, n_mp,
):
    images, tokens, d = block_input.shape
    groups = n_mp
    gh, table_len = pos_table.shape
    gc = gh * HD
    hid = fc1_bias.shape[0]
    heads = groups * gh
    rows_w = qkv_weight.shape[0]
    wpos = rel_index.shape[0]
    wins = tokens // wpos
    prow = wins * WPAD
    trow = -(-tokens // 16) * 16
    mine = images // n_mp
    imgs = 2 if mine % 2 == 0 else 1
    steps = mine // imgs
    off = (lax.axis_index("mp") * steps).astype(jnp.int32).reshape(1)

    small = jnp.concatenate(
        [qv_bias.reshape(-1), fc1_bias] + [p.reshape(-1).astype(BF16) for p in split3(pos_table)]
    )
    per_row = -(-small.shape[0] // rows_w)
    small = jnp.pad(small, (0, per_row * rows_w - small.shape[0])).reshape(rows_w, per_row)
    n_vec = norm_gains.shape[1] + offsets.shape[1]
    extra = -(-(per_row + n_vec) // 128) * 128
    pack_a = jnp.concatenate(
        [
            qkv_weight.reshape(rows_w, 3 * gc), norm_gains, offsets, small,
            jnp.zeros((rows_w, extra - per_row - n_vec), BF16),
        ],
        axis=1,
    )
    pack_b = jnp.concatenate([proj_weight, fc1_weight, fc2_weight], axis=1)

    def gather(pack):
        got = lax.all_gather(lax.all_gather(pack, "mp", axis=0, tiled=False), "dp", axis=1, tiled=True)
        return got

    wa = gather(pack_a)
    wb = gather(pack_b)
    vec = jnp.pad(wa[0, :, 3 * gc : 3 * gc + n_vec].astype(F32).T, ((0, 2), (0, 0)))
    small = wa[:, 0:rows_w, 3 * gc + n_vec : 3 * gc + n_vec + per_row].reshape(groups, -1).astype(F32)
    qvb = small[:, 0 : 2 * gc].reshape(groups, 2, gc).transpose(1, 0, 2).reshape(2, groups * gc)
    qvb = jnp.pad(qvb, ((0, 6), (0, 0)))
    hb = small[:, 2 * gc : 2 * gc + hid].reshape(groups, 1, hid)
    tab = small[:, 2 * gc + hid : 2 * gc + hid + 3 * gh * table_len].reshape(groups, 3, gh, table_len)
    table = (tab[:, 0] + tab[:, 1] + tab[:, 2]).reshape(heads, table_len)

    pad_w = WPAD - wpos
    rel_t = jnp.pad(rel_index.T, ((0, pad_w), (0, pad_w)), constant_values=-1)
    one_hot = (rel_t.reshape(-1)[None, :] == jnp.arange(table_len, dtype=jnp.int32)[:, None]).astype(F32)
    pos = jnp.dot(table, one_hot, precision=lax.Precision.HIGHEST).reshape(groups, gh, WPAD, WPAD)
    side_wins = SIDE // WIN
    labels = (
        region_ids.reshape(side_wins, WIN, side_wins, WIN).transpose(0, 2, 1, 3).reshape(wins, wpos)
    )
    pen = jnp.where(labels[:, :, None] == labels[:, None, :], 0.0, -100.0).astype(F32)
    pen = jnp.pad(pen, ((0, 0), (0, 0), (0, pad_w)))
    pen = jnp.pad(pen, ((0, 0), (0, pad_w), (0, 0)), constant_values=DEAD)
    bias = pos.transpose(0, 2, 1, 3)[:, None] + pen[None, :, :, None, :]
    bias = bias.reshape(groups, wins, WPAD, gh * WPAD)

    pick = pick_matrix(tokens)
    pick_pad = np.pad(pick, ((0, 0), (0, trow - tokens)))
    pm = jnp.asarray(pick, BF16)
    pmp = jnp.asarray(pick_pad, BF16)
    pmt = jnp.asarray(pick_pad.T, BF16)
    params = pltpu.CompilerParams(vmem_limit_bytes=60 * 1024 * 1024)
    img_spec = pl.BlockSpec((imgs, tokens, d), lambda i, o: (o[0] + i, 0, 0))
    out_img_spec = pl.BlockSpec((imgs, tokens, d), lambda i, o: (i, 0, 0))
    full = groups * gc

    def rows_spec(r, c):
        return pl.BlockSpec((r, c), lambda i, o: (i, 0))

    probs_spec = pl.BlockSpec((imgs * wins, groups, WPAD, gh * WPAD), lambda i, o: (i, 0, 0, 0))
    qkv, hw, probs, attn = pl.pallas_call(
        functools.partial(attention_kernel, imgs=imgs, groups=groups, gh=gh, prow=prow, trow=trow),
        out_shape=(
            jax.ShapeDtypeStruct((mine * prow, 3 * full), BF16),
            jax.ShapeDtypeStruct((mine * prow, d), BF16),
            jax.ShapeDtypeStruct((mine * wins, groups, WPAD, gh * WPAD), F32),
            jax.ShapeDtypeStruct((mine * trow, full), BF16),
        ),
        grid_spec=pltpu.PrefetchScalarGridSpec(
            num_scalar_prefetch=1,
            grid=(steps,),
            in_specs=[
                img_spec, whole(wa.shape), whole(vec.shape), whole(qvb.shape), whole(bias.shape),
                whole(pm.shape), whole(pmt.shape),
            ],
            out_specs=[
                rows_spec(imgs * prow, 3 * full), rows_spec(imgs * prow, d), probs_spec,
                rows_spec(imgs * trow, full),
            ],
            scratch_shapes=[pltpu.VMEM((imgs * prow, full), BF16)],
        ),
        compiler_params=params,
        name="attention_forward",
    )(off, block_input, wa, vec, qvb, bias, pm, pmt)

    rows = imgs * trow
    out, gx1, gwb, ghb, sums_b = pl.pallas_call(
        functools.partial(feed_kernel, imgs=imgs, groups=groups, gc=gc, trow=trow, tokens=tokens),
        out_shape=(
            jax.ShapeDtypeStruct((mine, tokens, d), BF16),
            jax.ShapeDtypeStruct((mine * trow, d), F32),
            jax.ShapeDtypeStruct(wb.shape, BF16),
            jax.ShapeDtypeStruct((groups, 1, hid), F32),
            jax.ShapeDtypeStruct((8, d), F32),
        ),
        grid_spec=pltpu.PrefetchScalarGridSpec(
            num_scalar_prefetch=1,
            grid=(steps,),
            in_specs=[
                img_spec, img_spec, rows_spec(rows, full), whole(wb.shape), whole(vec.shape),
                whole(hb.shape),
            ],
            out_specs=[
                out_img_spec, rows_spec(rows, d), whole(wb.shape), whole(hb.shape), whole((8, d)),
            ],
            scratch_shapes=[
                pltpu.VMEM((rows, d), F32), pltpu.VMEM((rows, d), F32), pltpu.VMEM((rows, d), BF16),
                pltpu.VMEM((d, rows), BF16), pltpu.VMEM((d, rows), BF16),
                pltpu.VMEM((rows, d), F32), pltpu.VMEM((rows, d), F32),
                pltpu.VMEM((d, full), F32), pltpu.VMEM((groups, d, hid), F32),
                pltpu.VMEM((groups, d, hid), F32),
            ],
        ),
        compiler_params=params,
        name="feed_forward",
    )(off, block_input, out_grad, attn, wb, vec, hb)

    wp_spec = pl.BlockSpec((groups, d, gc), lambda i, o: (0, 0, 0), pipeline_mode=pl.Buffered(1))
    gin, gwa, gtab, gqv, sums_c = pl.pallas_call(
        functools.partial(
            attention_back_kernel, imgs=imgs, groups=groups, gh=gh, prow=prow, trow=trow, tokens=tokens
        ),
        out_shape=(
            jax.ShapeDtypeStruct((mine, tokens, d), BF16),
            jax.ShapeDtypeStruct((groups, d, 3 * gc), BF16),
            jax.ShapeDtypeStruct((groups, WPAD, gh * WPAD), F32),
            jax.ShapeDtypeStruct((8, full), F32),
            jax.ShapeDtypeStruct((8, d), F32),
        ),
        grid_spec=pltpu.PrefetchScalarGridSpec(
            num_scalar_prefetch=1,
            grid=(steps,),
            in_specs=[
                img_spec, rows_spec(rows, d), rows_spec(imgs * prow, 3 * full),
                rows_spec(imgs * prow, d), probs_spec, whole(wa.shape), wp_spec, whole(vec.shape),
                whole(pmp.shape), whole(pmt.shape),
            ],
            out_specs=[
                out_img_spec, whole((groups, d, 3 * gc)), whole((groups, WPAD, gh * WPAD)),
                whole((8, full)), whole((8, d)),
            ],
            scratch_shapes=[
                pltpu.VMEM((imgs * prow, d), BF16), pltpu.VMEM((imgs * prow, full), BF16),
                pltpu.VMEM((imgs * prow, 3 * full), BF16), pltpu.VMEM((d, imgs * prow), BF16),
                pltpu.VMEM((3, d, full), F32),
            ],
        ),
        compiler_params=params,
        name="attention_backward",
    )(off, block_input, gx1, qkv, hw, probs, wa, wb, vec, pmp, pmt)

    block_output = lax.all_gather(out, "mp", axis=0, tiled=True)
    input_grad = lax.all_gather(gin, "mp", axis=0, tiled=True)

    def scatter(g):
        part = lax.psum_scatter(g, "dp", scatter_dimension=1, tiled=True)
        return lax.psum_scatter(part, "mp", scatter_dimension=0, tiled=True)[0].astype(F32)

    gb = scatter(gwb)
    ga = scatter(gwa)
    gtab = gtab.reshape(groups, WPAD, gh, WPAD).transpose(0, 2, 1, 3).reshape(heads, WPAD * WPAD)
    gtab = lax.dot_general(gtab, one_hot, (((1,), (1,)), ((), ())), precision=lax.Precision.HIGHEST)
    sizes = [gtab.size, 2 * full, groups * hid, 2 * d, 4 * d]
    smalls = jnp.concatenate(
        [
            gtab.reshape(-1), gqv[0:2].reshape(-1), ghb.reshape(-1),
            sums_c[0], sums_b[0], sums_c[1], sums_b[1], sums_b[2], sums_b[3],
        ]
    )
    smalls = lax.psum(smalls, ("dp", "mp"))
    ends = np.cumsum(sizes)
    me = lax.axis_index("mp")
    my_rows = lax.axis_index("dp") * rows_w
    table_grad = lax.dynamic_slice_in_dim(smalls[0 : ends[0]].reshape(heads, table_len), me * gh, gh, 0)
    qv_grad = lax.dynamic_slice_in_dim(smalls[ends[0] : ends[1]].reshape(2, full), me * gc, gc, 1)
    hb_grad = lax.dynamic_slice_in_dim(smalls[ends[1] : ends[2]], me * hid, hid, 0)
    gains_grad = lax.dynamic_slice_in_dim(smalls[ends[2] : ends[3]].reshape(2, d), my_rows, rows_w, 1).T
    offs_grad = lax.dynamic_slice_in_dim(smalls[ends[3] : ends[4]].reshape(4, d), my_rows, rows_w, 1).T
    return (
        block_output, input_grad, gains_grad, offs_grad, ga.reshape(rows_w, 3, gc), qv_grad,
        table_grad, gb[:, 0:gc], gb[:, gc : gc + hid], hb_grad, gb[:, gc + hid : gc + 2 * hid],
    )


def solution(mesh):
    in_specs = (
        P("dp", None, None), P("dp", None, None), P("dp", None), P("dp", None), P("dp", None, "mp"),
        P(None, "mp"), P("mp", None), P("dp", "mp"), P("dp", "mp"), P("mp"), P("dp", "mp"), P(), P(),
    )
    out_specs = (
        P("dp", None, None), P("dp", None, None), P("dp", None), P("dp", None), P("dp", None, "mp"),
        P(None, "mp"), P("mp", None), P("dp", "mp"), P("dp", "mp"), P("mp"), P("dp", "mp"),
    )
    body = functools.partial(shards, n_dp=mesh.shape["dp"], n_mp=mesh.shape["mp"])
    return jax.shard_map(body, mesh=mesh, in_specs=in_specs, out_specs=out_specs, check_vma=False)
```

time: 1230 us -> 507 us (0.41); the launches traced: 1210 us -> 506 us
  waiting for transfers between devices: 643 us -> 266 us
  local copies, waits for them, and re-layouts: 245 us -> 44.2 us
  other arithmetic: 128 us -> 4.31 us
  matrix products: 109 us -> 4.41 us
  Pallas kernels: 0 us -> 99.7 us
    psum x3 -> x0, waiting for transfers between devices: 601 us -> none  [the longest x1 333 us: shards(): lax.psum(along_cols(act_rows, fc2_w).astype(jnp.bfloat16), 'mp')]
    all_gather x0 -> x4, waiting for transfers between devices: none -> 156 us  [the longest x1 86.3 us: shards(): block_output = lax.all_gather(out, 'mp', axis=0, tiled=True)]
    dot_general x28 -> x2, matrix products: 109 us -> 4.41 us  [the longest x1 3.01 us: shards(): jnp.dot(table, one_hot, precision=lax.Precision.HIGHEST)]
    pallas_call x0 -> x3, Pallas kernels: none -> 99.7 us  [the longest x1 39.1 us: shards(): pl.pallas_call(functools.partial(attention_back_kernel, imgs=imgs, groups...]
    reduce_scatter x4, waiting for transfers between devices: 18.8 us -> 108 us  [the longest x2 91.5 us: scatter(): part = lax.psum_scatter(g, 'dp', scatter_dimension=1, tiled=True)]
    another operation x17 -> x0, local copies, waits for them, and re-layouts: 72.9 us -> none  [the longest x6 47.7 us: shards(): jnp.stack([grad_q, grad_k, grad_v], axis=1).astype(jnp.bfloat16)]
    reduce_sum x19 -> x0, other arithmetic: 71.7 us -> none  [the longest x2 10.7 us: layer_norm(): row_mean = jnp.mean(values, axis=-1, keepdims=True)]
    convert_element_type x19 -> x2, other arithmetic: 44.8 us -> 1.63 us  [the longest x1 0.93 us: scatter(): lax.psum_scatter(part, 'mp', scatter_dimension=0, tiled=True)[0].astype(F32)]
  transfers between devices with their start and end apart: 9 -> 8, of which waited for: 5 -> 6; matrix products, arithmetic and copies ran while one was open for 23% -> 9% of each run, Pallas kernels for 0% -> 5%
where the time goes in v1:
time: 507 us; the launch traced here: 506 us
  waiting for transfers between devices  266 us (52%)
  Pallas kernels  99.7 us (20%)
  blocking collectives  72.5 us (14%)
  local copies, waits for them, and re-layouts  44.2 us (9%)
  between operations  14.4 us (3%)
    reduce_scatter x2, waiting for transfers between devices, scatter(): part = lax.psum_scatter(g, 'dp', scatter_dimension=1, tiled=True)  91.5 us
    all_gather x1, waiting for transfers between devices, shards(): block_output = lax.all_gather(out, 'mp', axis=0, tiled=True)  86.3 us
    all_gather x1, waiting for transfers between devices, shards(): input_grad = lax.all_gather(gin, 'mp', axis=0, tiled=True)  68.5 us
    psum x1, blocking collectives, shards(): smalls = lax.psum(smalls, ('dp', 'mp'))  39.6 us
    pallas_call x1, Pallas kernels, shards(): pl.pallas_call(functools.partial(attention_back_kernel, imgs=imgs, groups...  39.1 us
    pallas_call x1, Pallas kernels, shards(): pl.pallas_call(functools.partial(feed_kernel, imgs=imgs, groups=groups, g...  33.9 us
    all_gather x2, blocking collectives, gather(): lax.all_gather(pack, 'mp', axis=0, tiled=False)  32.8 us
    unnamed x30, local copies, waits for them, and re-layouts  27 us
  transfers between devices with their start and end apart: 8, of which 6 were waited for; matrix products, arithmetic and copies ran while one was open for 9% of the time, Pallas kernels for 5%

profile of v1, /device:TPU:0, one launch (start us, length us, event | category | flops | bytes accessed | tf_op | source)
XLA Modules:
  0.0 506.2 jit_solution(5281648460834966278)
XLA Ops:
  8.2 1.4 concatenate.12
  9.8 0.8 copy.88
  10.5 0.8 copy.89
  11.5 15.7 %all-gather = bf16[256,512]{1,0:T(8,128)(2,1)S(1)} all-gather(bf16[64,512]{1,0:T(8,128)(2,1)S(1)} %concatenate.13), channel_id=2, replica_groups=mesh['dp'=8,'mp'=4] {'mp'}, dimensions={0}, use_global_device_ids=true | all-gather | bytes 327680 | tf_op jit(solution)/shard_map/all_gather | solution.py:332
  27.1 0.9 copy.90
  28.1 0.9 pad_maximum_fusion
  29.0 17.2 %all-gather.1 = bf16[256,1152]{1,0:T(8,128)(2,1)} all-gather(bf16[64,1152]{1,0:T(8,128)(2,1)S(1)} %pad_maximum_fusion), channel_id=3, replica_groups=mesh['dp'=8,'mp'=4] {'mp'}, dimensions={0}, use_global_device_ids=true | all-gather | bytes 737280 | tf_op jit(solution)/shard_map/all_gather | solution.py:332
  46.3 0.8 reshape.135
  47.1 0.8 copy.117
  48.6 6.5 %copy.102.x_ref = bf16[24,196,512]{2,1,0:T(8,128)(2,1)} copy(bf16[24,196,512]{2,0,1:T(8,128)(2,1)} %param.16) | data formatting | bytes 9633792 | tf_op args[0]
  55.1 3.9 copy.103.gy_ref
  59.0 1.1 slice.93
  61.2 1.2 slice.92
  62.6 3.0 fusion.6
  66.5 1.8 copy.101.w_ref.wa_ref
  68.9 1.1 broadcast_add_fusion.bias_ref
  70.0 26.7 %attention_forward.1 = (bf16[1536,1536]{1,0:T(8,128)(2,1)}, bf16[1536,512]{1,0:T(8,128)(2,1)}, f32[24,4,64,256]{3,2,1,0:T(8,128)}, bf16[1248,512]{1,0:T(8,128)(2,1)}) custom-call(s32[1]{0:T(128)} %bitcast.off_ref, bf16[24,196,512]{2,1,0:T(8,128)(2,1)} %copy.102.x_ref, bf16[4,512,512]{2,1,0:T(8,128)(2,1)} %copy.101.w_ref.wa_ref, ...), custom_call_target="tpu_custom_call" | custom-call | tf_op jit(solution)/shard_map/attention_forward/pallas_call | solution.py:373
  96.8 1.5 all-gather.9.cloned.1.call-done.w_ref.wp_ref
  98.3 33.9 %feed_forward.1 = (bf16[6,196,512]{2,1,0:T(8,128)(2,1)}, f32[1248,512]{1,0:T(8,128)}, bf16[4,512,1152]{2,1,0:T(8,128)(2,1)}, f32[4,1,512]{2,1,0:T(1,128)}, f32[8,512]{1,0:T(8,128)}) custom-call(s32[1]{0:T(128)} %bitcast.off_ref, bf16[24,196,512]{2,1,0:T(8,128)(2,1)} %copy.102.x_ref, bf16[24,196,512]{2,1,0:T(8,128)(2,1)} %copy.103.gy_ref, ...), custom_call_target="tpu_custom_call" | custom-call | tf_op jit(solution)/shard_map/feed_forward/pallas_call | solution.py:399
  132.2 39.1 %attention_backward.1 = (bf16[6,196,512]{2,1,0:T(8,128)(2,1)}, bf16[4,512,384]{2,1,0:T(8,128)(2,1)}, f32[4,64,256]{2,1,0:T(8,128)}, f32[8,512]{1,0:T(8,128)}, f32[8,512]{1,0:T(8,128)}) custom-call(s32[1]{0:T(128)} %bitcast.off_ref, bf16[24,196,512]{2,1,0:T(8,128)(2,1)} %copy.102.x_ref, f32[1248,512]{1,0:T(8,128)} %get-tuple-element.27.gx1_ref, ...), custom_call_target="tpu_custom_call" | custom-call | tf_op jit(solution)/shard_map/attention_backward/pallas_call | solution.py:431
  172.0 37.8 %reduce-scatter.5.cloned.1.call-done = bf16[4,64,384]{2,1,0:T(8,128)(2,1)} async-done(((bf16[4,512,384]{2,1,0:T(8,128)(2,1)}), bf16[4,64,384]{2,1,0:T(8,128)(2,1)}) %reduce-scatter.5.cloned.1.call-update) | async-done | bytes 196624 | tf_op jit(solution)/shard_map/reduce_scatter | solution.py:468
  212.5 1.4 fusion.3
  213.9 53.6 %reduce-scatter.9.cloned.1.call-done = bf16[4,64,1152]{2,1,0:T(8,128)(2,1)} async-done(((bf16[4,512,1152]{2,1,0:T(8,128)(2,1)}), bf16[4,64,1152]{2,1,0:T(8,128)(2,1)}) %reduce-scatter.9.cloned.1.call-update) | async-done | bytes 589840 | tf_op jit(solution)/shard_map/reduce_scatter | solution.py:468
  267.6 0.8 fusion.19
  268.6 39.6 %psum.7 = f32[8848]{0:T(1024)S(1)} all-reduce(f32[8848]{0:T(1024)S(1)} %concatenate.15), channel_id=1, replica_groups=mesh['dp'=8,'mp'=4] {'dp','mp'}, use_global_device_ids=true, to_apply=%region_0.1 | all-reduce | flops 8848 | bytes 70784 | tf_op jit(solution)/shard_map/psum | solution.py:482
  311.6 0.8 reshape.147
  313.1 68.5 %all-gather.13.cloned.1.call-done = bf16[24,196,512]{2,1,0:T(8,128)(2,1)} async-done(((bf16[6,196,512]{2,1,0:T(8,128)(2,1)}), bf16[24,196,512]{2,1,0:T(8,128)(2,1)}) %all-gather.13.cloned.1.call-update) | async-done | bytes 4816912 | tf_op jit(solution)/shard_map/all_gather | solution.py:465
  381.6 6.3 %copy.109 = bf16[24,196,512]{2,0,1:T(8,128)(2,1)} copy(bf16[24,196,512]{2,1,0:T(8,128)(2,1)} %all-gather.13.cloned.1.call-done) | data formatting | bytes 9633792
  387.8 86.3 %all-gather.11.cloned.1.call-done = bf16[24,196,512]{2,1,0:T(8,128)(2,1)} async-done(((bf16[6,196,512]{2,1,0:T(8,128)(2,1)}), bf16[24,196,512]{2,1,0:T(8,128)(2,1)}) %all-gather.11.cloned.1.call-update) | async-done | bytes 4816912 | tf_op jit(solution)/shard_map/all_gather | solution.py:464
  474.2 6.3 %copy.108 = bf16[24,196,512]{2,0,1:T(8,128)(2,1)} copy(bf16[24,196,512]{2,1,0:T(8,128)(2,1)} %all-gather.11.cloned.1.call-done) | data formatting | bytes 9633792
  480.4 16.6 %reduce-scatter.11.cloned.1.call-done = bf16[1,64,1152]{2,1,0:T(8,128)(2,1)} async-done(((bf16[4,64,1152]{2,1,0:T(8,128)(2,1)}), bf16[1,64,1152]{2,1,0:T(8,128)(2,1)}) %reduce-scatter.11.cloned.1.call-update) | async-done | bytes 147472 | tf_op jit(solution)/shard_map/reduce_scatter | solution.py:469
  497.1 0.9 bitcast_convert_fusion
  (88 shorter events, 13.6 us)
Async XLA Ops:
  7.2 4.2 copy-start
  7.2 51.7 %all-gather.7.cloned.1.call-start = ((), (), s32[]{:S(2)}) async-start(), calls=%async_computation.4 | async-start | bytes 2359296 | tf_op jit(solution)/shard_map/all_gather | solution.py:332
  28.1 70.2 %all-gather.9.cloned.1.call-start = ((), (), s32[]{:S(2)}) async-start(), calls=%async_computation.5 | async-start | bytes 5308416 | tf_op jit(solution)/shard_map/all_gather | solution.py:332
  46.2 163.6 %reduce-scatter.5.cloned.1.call-start = ((), (), s32[]{:S(2)}) async-start(), calls=%async_computation.8 | async-start | bytes 1769472 | tf_op jit(solution)/shard_map/reduce_scatter | solution.py:468
  48.2 6.8 %slice-start = ((s8[4816896]{0:T(1024)(128)(4,1)}), s8[622592]{0:T(1024)(128)(4,1)S(1)}, s32[]{:S(2)}) async-start(s8[4816896]{0:T(1024)(128)(4,1)} %bitcast.80), calls=%async_computation.12 | async-start | bytes 1245184
  48.6 6.5 %slice-start.1 = ((s8[4816896]{0:T(1024)(128)(4,1)}), s8[4194304]{0:T(1024)(128)(4,1)S(1)}, s32[]{:S(2)}) async-start(s8[4816896]{0:T(1024)(128)(4,1)} %bitcast.80), calls=%async_computation.13 | async-start | bytes 8388608
  58.9 7.6 %copy-start.2 = (bf16[4,512,512]{2,0,1:T(4,128)(2,1)S(1)}, bf16[4,512,512]{2,0,1:T(4,128)(2,1)}, u32[]{:S(2)}) copy-start(bf16[4,512,512]{2,0,1:T(4,128)(2,1)} %all-gather.7.cloned.1.call-done) | copy-start | bytes 6291460
  171.3 40.0 %copy-start.3 = (f32[4,64,256]{2,1,0:T(8,128)S(1)}, f32[4,64,256]{2,1,0:T(8,128)}, u32[]{:S(2)}) copy-start(f32[4,64,256]{2,1,0:T(8,128)} %get-tuple-element.32) | copy-start | bytes 786436
  171.4 96.2 %reduce-scatter.9.cloned.1.call-start = ((), (), s32[]{:S(2)}) async-start(), calls=%async_computation.10 | async-start | bytes 5308416 | tf_op jit(solution)/shard_map/reduce_scatter | solution.py:468
  171.4 97.1 %copy-start.5 = (f32[8,512]{1,0:T(8,128)S(1)}, f32[8,512]{1,0:T(8,128)}, u32[]{:S(2)}) copy-start(f32[8,512]{1,0:T(8,128)} %get-tuple-element.36) | copy-start | bytes 49156
  171.4 97.1 %copy-start.4 = (f32[4,1,512]{2,1,0:T(1,128)S(1)}, f32[4,1,512]{2,1,0:T(1,128)}, u32[]{:S(2)}) copy-start(f32[4,1,512]{2,1,0:T(1,128)} %get-tuple-element.34) | copy-start | bytes 24580
  171.9 139.7 %reduce-scatter.7.cloned.1.call-start = ((), (), s32[]{:S(2)}) async-start(), calls=%async_computation.9 | async-start | bytes 245760 | tf_op jit(solution)/shard_map/reduce_scatter | solution.py:469
  209.8 171.8 %all-gather.13.cloned.1.call-start = ((), (), s32[]{:S(2)}) async-start(), calls=%async_computation.7 | async-start | bytes 6144000 | tf_op jit(solution)/shard_map/all_gather | solution.py:465
  210.4 263.8 %all-gather.11.cloned.1.call-start = ((), (), s32[]{:S(2)}) async-start(), calls=%async_computation.6 | async-start | bytes 6144000 | tf_op jit(solution)/shard_map/all_gather | solution.py:464
  211.1 285.9 %reduce-scatter.11.cloned.1.call-start = ((), (), s32[]{:S(2)}) async-start(), calls=%async_computation.11 | async-start | bytes 737280 | tf_op jit(solution)/shard_map/reduce_scatter | solution.py:469
  381.6 117.8 %copy-start.1 = (bf16[64,3,128]{2,0,1:T(8,128)(2,1)S(1)}, bf16[64,3,128]{2,0,1:T(8,128)(2,1)}, u32[]{:S(2)}) copy-start(bf16[64,3,128]{2,0,1:T(8,128)(2,1)} %param.20) | copy-start | bytes 147460
Sparse Core Ops, SparseCore 0:
  28.2 29.3 all-gather.6
  59.4 38.8 all-gather.8
  171.5 38.2 reduce-scatter.4
  213.7 53.8 reduce-scatter.8
  269.6 19.5 reduce-scatter.6
  290.7 90.8 all-gather.12
  383.1 91.0 all-gather.10
  476.5 20.5 reduce-scatter.10

commit v2 on v1

v2 whole, which is shorter than its diff:
```python
import functools
import math

import jax
import jax.numpy as jnp
import numpy as np
from jax import lax
from jax.experimental import pallas as pl
from jax.experimental.pallas import tpu as pltpu
from jax.sharding import PartitionSpec as P

HD = 32
WIN = 7
SHIFT = 3
SIDE = 14
F32 = jnp.float32
BF16 = jnp.bfloat16
WPAD = 64
EPS = 1e-05
DEAD = -1e30


def dot(a, b, ca=1, cb=0):
    return lax.dot_general(a, b, (((ca,), (cb,)), ((), ())), preferred_element_type=F32)


def padded_order(shift):
    sides = SIDE // WIN
    wpos = WIN * WIN
    rows = np.full((sides * sides * WPAD,), -1, np.int32)
    for wr in range(sides):
        for wc in range(sides):
            for a in range(wpos):
                r = (wr * WIN + a // WIN + shift) % SIDE
                c = (wc * WIN + a % WIN + shift) % SIDE
                rows[(wr * sides + wc) * WPAD + a] = r * SIDE + c
    return rows


def pick_matrix(tokens, shift=SHIFT):
    rows = padded_order(shift)
    return (rows[:, None] == np.arange(tokens)[None, :]).astype(np.float32)


def norm(x):
    mean = jnp.mean(x, axis=-1, keepdims=True)
    cen = x - mean
    var = jnp.mean(cen * cen, axis=-1, keepdims=True)
    inv = lax.rsqrt(var + EPS)
    return cen * inv, inv


def norm_back(grad, normed, inv, gain):
    scaled = grad * gain
    return inv * (
        scaled
        - jnp.mean(scaled, axis=-1, keepdims=True)
        - normed * jnp.mean(scaled * normed, axis=-1, keepdims=True)
    )


def col_sum(v):
    return jnp.sum(v, axis=0, keepdims=True)


def head_masks(group_heads):
    lane_q = lax.broadcasted_iota(jnp.int32, (group_heads * WPAD, group_heads * HD), 0)
    lane_c = lax.broadcasted_iota(jnp.int32, (group_heads * WPAD, group_heads * HD), 1)
    return (lane_q // WPAD) == (lane_c // HD)


def spread(rows, mask, group_heads):
    tiled = jnp.concatenate([rows] * group_heads, axis=0)
    return jnp.where(mask, tiled, jnp.zeros_like(tiled))


def gather_heads(full, mask, group_heads):
    kept = jnp.where(mask, full, 0.0)
    total = kept[0:WPAD]
    for h in range(1, group_heads):
        total = total + kept[h * WPAD : (h + 1) * WPAD]
    return total


def vectors(vec_ref):
    return vec_ref[0].astype(F32).T


def attention_kernel(
    x_ref, w_ref, vec_ref, sm_ref, pos_ref, pen_ref, pm_ref, pmt_ref,
    *rest, imgs, groups, gh, prow, trow,
):
    qkv_ref, hw_ref, probs_ref, attn_ref, attw = rest[-5:]
    gc = gh * HD
    full = groups * gc
    vec = vectors(vec_ref)
    gain = vec[0:1, :]
    shift = vec[2:3, :]
    q_bias = jnp.concatenate([sm_ref[g, 0:1, :] for g in range(groups)], axis=1)
    v_bias = jnp.concatenate([sm_ref[g, 1:2, :] for g in range(groups)], axis=1)
    for im in range(imgs):
        normed, _ = norm(x_ref[im].astype(F32))
        h1 = (normed * gain + shift).astype(BF16)
        hw_ref[im * prow : (im + 1) * prow, :] = dot(pm_ref[...], h1).astype(BF16)
    hw = hw_ref[...]
    for kind in range(3):
        wk = jnp.concatenate([w_ref[g, :, kind * gc : (kind + 1) * gc] for g in range(groups)], axis=1)
        part = dot(hw, wk)
        if kind == 0:
            part = (part + q_bias) * (HD**-0.5)
        if kind == 2:
            part = part + v_bias
        qkv_ref[:, kind * full : (kind + 1) * full] = part.astype(BF16)
    wins = prow // WPAD
    mask = head_masks(gh)

    def window(i, carry):
        rows = pl.ds(pl.multiple_of(i * WPAD, WPAD), WPAD)
        win = lax.rem(i, wins)
        for g in range(groups):
            q = qkv_ref[rows, g * gc : (g + 1) * gc]
            k = qkv_ref[rows, full + g * gc : full + (g + 1) * gc]
            v = qkv_ref[rows, 2 * full + g * gc : 2 * full + (g + 1) * gc]
            scores = dot(k, spread(q, mask, gh), 1, 1) + (pos_ref[g] + pen_ref[win])
            e = jnp.exp(scores - jnp.max(scores, axis=0, keepdims=True))
            p = e * (1.0 / jnp.sum(e, axis=0, keepdims=True))
            probs_ref[i, g] = p
            o = gather_heads(dot(p.astype(BF16), v, 0, 0), mask, gh)
            attw[rows, g * gc : (g + 1) * gc] = o.astype(BF16)
        return carry

    lax.fori_loop(0, imgs * wins, window, 0)
    for im in range(imgs):
        attn_ref[im * trow : (im + 1) * trow, :] = dot(
            pmt_ref[...], attw[im * prow : (im + 1) * prow, :]
        ).astype(BF16)


def gelu_parts(pre):
    cdf = 0.5 * (1.0 + lax.erf(pre * (1.0 / math.sqrt(2.0))))
    density = jnp.exp(-0.5 * pre * pre) * (1.0 / math.sqrt(2.0 * math.pi))
    return pre * cdf, cdf + pre * density


def feed_kernel(
    x_ref, gy_ref, attn_ref, w_ref, vec_ref, sm_ref,
    *rest, imgs, groups, gc, hid, trow, tokens,
):
    out_ref, gx1_ref, act_ref, gpb_ref, h2_ref, gyp_ref, gb_ref, sums_ref, xs, gys, mlp, gh2 = rest[-12:]
    vec = vectors(vec_ref)

    @pl.when(pl.program_id(0) == 0)
    def _():
        gb_ref[...] = jnp.zeros_like(gb_ref)
        sums_ref[...] = jnp.zeros_like(sums_ref)

    xs[...] = jnp.zeros_like(xs)
    gys[...] = jnp.zeros_like(gys)
    for im in range(imgs):
        xs[im * trow : im * trow + tokens, :] = x_ref[im].astype(F32)
        gys[im * trow : im * trow + tokens, :] = gy_ref[im].astype(F32)
    proj = jnp.concatenate([w_ref[g, :, 0:gc] for g in range(groups)], axis=1)
    x1 = xs[...] + dot(attn_ref[...], proj, 1, 1) + vec[3:4, :]
    xs[...] = x1
    normed2, inv2 = norm(x1)
    h2_ref[...] = (normed2 * vec[1:2, :] + vec[4:5, :]).astype(BF16)
    gyp_ref[...] = gys[...].astype(BF16)
    mlp[...] = jnp.zeros_like(mlp)
    gh2[...] = jnp.zeros_like(gh2)

    for g in range(groups):
        fc1 = w_ref[g, :, gc : gc + hid]
        fc2 = w_ref[g, :, gc + hid : gc + 2 * hid]
        pre = dot(h2_ref[...], fc1) + jnp.concatenate(
            [sm_ref[g, 2 + k : 3 + k, :] for k in range(hid // 128)], axis=1
        )
        act, slope = gelu_parts(pre)
        act = act.astype(BF16)
        act_ref[:, g * hid : (g + 1) * hid] = act
        gpre = dot(gyp_ref[...], fc2) * slope
        gpb = gpre.astype(BF16)
        gpb_ref[:, g * hid : (g + 1) * hid] = gpb
        gb_ref[g] += col_sum(gpre)
        mlp[...] += dot(act, fc2, 1, 1)
        gh2[...] += dot(gpb, fc1, 1, 1)

    out = xs[...] + mlp[...] + vec[5:6, :]
    for im in range(imgs):
        out_ref[im] = out[im * trow : im * trow + tokens].astype(BF16)
    normed2, inv2 = norm(xs[...])
    grad = gh2[...]
    gy = gys[...]
    gx1 = gy + norm_back(grad, normed2, inv2, vec[1:2, :])
    gx1_ref[...] = gx1
    sums_ref[0:1, :] += col_sum(grad * normed2)
    sums_ref[1:2, :] += col_sum(gx1)
    sums_ref[2:3, :] += col_sum(grad)
    sums_ref[3:4, :] += col_sum(gy)


def attention_back_kernel(
    x_ref, gx1_ref, qkv_ref, probs_ref, wa_ref, wp_ref, vec_ref, pm_ref, pmt_ref,
    gin_ref, gqkv, table_ref, qvs_ref, sums_ref,
    gxw, ga, *, imgs, groups, gh, prow, trow, tokens, middle,
):
    step = pl.program_id(0)
    gc = gh * HD
    full = groups * gc

    gain = vectors(vec_ref)[0:1, :]

    @pl.when(step == 0)
    def _():
        table_ref[...] = jnp.zeros_like(table_ref)
        qvs_ref[...] = jnp.zeros_like(qvs_ref)
        sums_ref[...] = jnp.zeros_like(sums_ref)

    for im in range(imgs):
        gxw[im * prow : (im + 1) * prow, :] = dot(
            pm_ref[...], gx1_ref[im * trow : (im + 1) * trow, :].astype(BF16)
        ).astype(BF16)
    proj = jnp.concatenate([wp_ref[g, :, 0:gc] for g in range(groups)], axis=1)
    ga[...] = dot(gxw[...], proj).astype(BF16)
    mask = head_masks(gh)
    wins = prow // WPAD

    def window(i, carry):
        rows = pl.ds(pl.multiple_of(i * WPAD, WPAD), WPAD)
        all_rows = pl.ds(pl.multiple_of(step * imgs * prow + i * WPAD, WPAD), WPAD)
        for g in range(groups):
            cols = slice(g * gc, (g + 1) * gc)
            q = qkv_ref[rows, g * gc : (g + 1) * gc]
            k = qkv_ref[rows, full + g * gc : full + (g + 1) * gc]
            v = qkv_ref[rows, 2 * full + g * gc : 2 * full + (g + 1) * gc]
            p = probs_ref[i, g]
            gas = spread(ga[rows, cols], mask, gh)
            dp = dot(v, gas, 1, 1)
            ds = p * (dp - jnp.sum(p * dp, axis=0, keepdims=True))
            table_ref[g] += ds
            dsb = ds.astype(BF16)
            gq = gather_heads(dot(dsb, k, 0, 0), mask, gh) * (HD**-0.5)
            gk = dot(dsb, spread(q, mask, gh))
            gv = dot(p.astype(BF16), gas)
            qvs_ref[0:1, cols] += col_sum(gq)
            qvs_ref[1:2, cols] += col_sum(gv)
            gqkv[0, all_rows, cols] = gq.astype(BF16)
            gqkv[1, all_rows, cols] = gk.astype(BF16)
            gqkv[2, all_rows, cols] = gv.astype(BF16)
        return carry

    lax.fori_loop(0, imgs * wins, window, 0)
    middle()
    now = pl.ds(pl.multiple_of(step * imgs * prow, prow), imgs * prow)
    gh1 = None
    for kind in range(3):
        wk = jnp.concatenate([wa_ref[g, :, kind * gc : (kind + 1) * gc] for g in range(groups)], axis=1)
        term = dot(gqkv[kind, now, :], wk, 1, 1)
        gh1 = term if gh1 is None else gh1 + term
    gh1b = gh1.astype(BF16)
    for im in range(imgs):
        grad = dot(pmt_ref[...], gh1b[im * prow : (im + 1) * prow])[0:tokens]
        normed, inv = norm(x_ref[im].astype(F32))
        sums_ref[0:1, :] += col_sum(grad * normed)
        sums_ref[1:2, :] += col_sum(grad)
        gx0 = gx1_ref[im * trow : im * trow + tokens, :] + norm_back(grad, normed, inv, gain)
        gin_ref[im] = gx0.astype(BF16)


class Relay:
    def __init__(self, src, dst, sems, n_mp, passed):
        self.src, self.dst, self.n, self.passed = src, dst, n_mp, passed
        self.own_sem, self.send_sem, self.recv_sem, self.far_sem = sems
        self.m, self.me = lax.axis_index("mp"), lax.axis_index("dp")
        self.pieces = src.shape[0]

    @staticmethod
    def scratch(pieces, n_mp):
        dma = pltpu.SemaphoreType.DMA
        return [dma, dma((n_mp, pieces, 2)), dma((n_mp, pieces)), dma((n_mp, pieces))]

    def copy(self, s, p, step, own):
        return pltpu.make_async_remote_copy(
            src_ref=self.src.at[p] if own else self.dst.at[s, p], dst_ref=self.dst.at[s, p],
            send_sem=self.send_sem.at[s, p, (step + 1) // 2], recv_sem=self.recv_sem.at[s, p],
            device_id=(self.me, self.m + step), device_id_type=pl.DeviceIdType.MESH,
        )

    def far(self, p, j):
        to = lax.rem(self.m + j, self.n)
        return pltpu.make_async_remote_copy(
            src_ref=self.src.at[p], dst_ref=self.dst.at[self.m, p], send_sem=self.far_sem.at[j, p],
            recv_sem=self.recv_sem.at[self.m, p], device_id=(self.me, to),
            device_id_type=pl.DeviceIdType.MESH,
        )

    def edge(self, step):
        return self.m < self.n - 1 if step == 1 else self.m > 0

    def own_copy(self):
        return pltpu.make_async_copy(self.src, self.dst.at[self.m], self.own_sem)

    def start(self, greet=True):
        if greet:
            barrier = pltpu.get_barrier_semaphore()
            for j in range(1, self.n):
                pl.semaphore_signal(
                    barrier, inc=1, device_id=(self.me, lax.rem(self.m + j, self.n)),
                    device_id_type=pl.DeviceIdType.MESH,
                )
            pl.semaphore_wait(barrier, self.n - 1)
        for p in range(self.passed):
            for step in (1, -1):
                pl.when(self.edge(step))(lambda p=p, step=step: self.copy(self.m, p, step, True).start())
        for p in range(self.passed, self.pieces):
            for j in range(1, self.n):
                self.far(p, j).start()
        self.own_copy().start()

    def arrivals(self, k):
        return ((self.m - k, 1, self.m - k >= 0), (self.m + k, -1, self.m + k < self.n))

    def pass_one(self, k, p):
        for s, step, there in self.arrivals(k):

            def go(s=s, step=step):
                self.copy(s, p, step, False).wait_recv()
                pl.when(self.edge(step))(lambda: self.copy(s, p, step, False).start())

            pl.when(there)(go)

    def pass_on(self, k):
        for p in range(self.passed):
            self.pass_one(k, p)

    def finish(self):
        self.own_copy().wait()
        for p in range(self.passed, self.pieces):
            for j in range(1, self.n):
                self.far(p, j).wait_send()
                self.copy(lax.rem(self.m + j, self.n), p, 1, False).wait_recv()
        for p in range(self.passed):
            for step in (1, -1):
                pl.when(self.edge(step))(lambda p=p, step=step: self.copy(self.m, p, step, True).wait_send())
            for k in range(1, self.n):
                for s, step, there in self.arrivals(k):
                    pl.when(there & self.edge(step))(
                        lambda s=s, step=step, p=p: self.copy(s, p, step, False).wait_send()
                    )


def forward_kernel(*refs, imgs, groups, gh, gc, hid, prow, trow, tokens, kept, n_mp, relayed):
    refs = list(refs)
    x, gy, wa, wb, vec, sm, pos, pen, pm, pmt = refs[:10]
    refs = refs[10 + kept :]
    source = refs.pop(0) if relayed else None
    qkv, hw, probs, attn, out, gx1, act, gpb, h2, gyp, gb, sums = refs[:12]
    refs = refs[12:]
    target = refs.pop(0) if relayed else None
    attw, xs, gys, mlp, gh2 = refs[:5]
    step = pl.program_id(0)
    last = pl.num_programs(0) - 1
    relay = Relay(source, target, refs[5:], n_mp, 0) if relayed else None

    if relayed:
        pl.when(step == 0)(relay.start)
    attention_kernel(
        x, wa, vec, sm, pos, pen, pm, pmt, qkv, hw, probs, attn, attw,
        imgs=imgs, groups=groups, gh=gh, prow=prow, trow=trow,
    )
    feed_kernel(
        x, gy, attn, wb, vec, sm, out, gx1, act, gpb, h2, gyp, gb, sums, xs, gys, mlp, gh2,
        imgs=imgs, groups=groups, gc=gc, hid=hid, trow=trow, tokens=tokens,
    )
    if relayed:
        pl.when(step == last)(relay.finish)


def backward_kernel(*refs, imgs, steps, groups, gh, gc, hid, prow, trow, tokens, n_mp):
    refs = list(refs)
    x, gx1, qkv, probs, wa, wp, vec, pmp, pmt = refs[:9]
    hw, gx1_all, attn, h2, gpb, gyp, act, sums_1, sums_2, source = refs[9:19]
    gin, table, qvs, gw, target = refs[19:24]
    gqkv, sums, gxw, ga, vsum, hwt, gxt, h2t, gyt = refs[24:33]
    relay = Relay(source, target, refs[33:], n_mp, source.shape[0])
    todo = [(k, p) for k in range(1, n_mp) for p in range(relay.pieces)]

    def hook(at):
        return lambda: relay.pass_one(*todo[at])

    placed = max(0, min(2 * steps - 1, len(todo) - relay.pieces))

    def middle():
        for j in range(1, steps):
            if 2 * j - 1 < placed:
                pl.when(step == j)(hook(2 * j - 1))

    step = pl.program_id(0)

    @pl.when(step == 0)
    def _():
        relay.start()

    @pl.when(step < steps)
    def _():
        attention_back_kernel(
            x, gx1, qkv, probs, wa, wp, vec, pmp, pmt, gin, gqkv, table, qvs, sums, gxw, ga,
            imgs=imgs, groups=groups, gh=gh, prow=prow, trow=trow, tokens=tokens, middle=middle,
        )

    for j in range(steps):
        if 2 * j < placed:
            pl.when(step == j)(hook(2 * j))

    @pl.when(step >= steps)
    def _():
        g = step - steps

        @pl.when(g == 0)
        def _():
            hwt[...] = hw[...].astype(F32).T.astype(BF16)
            gxt[...] = gx1_all[...].T.astype(BF16)
            h2t[...] = h2[...].astype(F32).T.astype(BF16)
            gyt[...] = gyp[...].astype(F32).T.astype(BF16)
            vsum[...] = jnp.zeros_like(vsum)
            vsum[0:1, :] = sums[0:1, :]
            vsum[1:2, :] = sums_1[0:1, :] + sums_2[0:1, :]
            vsum[2:3, :] = sums[1:2, :]
            vsum[3:6, :] = sums_1[1:4, :] + sums_2[1:4, :]

        cols = pl.ds(pl.multiple_of(g * gc, gc), gc)
        for kind in range(3):
            gw[0, :, kind * gc : (kind + 1) * gc] = dot(hwt[...], gqkv[kind, :, cols]).astype(BF16)
        at = 3 * gc
        gw[0, :, at : at + gc] = dot(gxt[...], attn[...]).astype(BF16)
        at += gc
        gw[0, :, at : at + hid] = dot(h2t[...], gpb[...]).astype(BF16)
        at += hid
        gw[0, :, at : at + hid] = dot(gyt[...], act[...]).astype(BF16)
        at += hid
        gw[0, :, at : at + vsum.shape[0]] = vsum[...].T.astype(BF16)

    @pl.when(step == steps + groups - 1)
    def _():
        for k, p in todo[placed:]:
            relay.pass_one(k, p)
        relay.finish()


def coords(n_dp):
    nb = n_dp.bit_length() - 1
    me = lax.axis_index("dp")
    return nb, me, [(me // (1 << (nb - 1 - p))) % 2 for p in range(nb)]


def flipped(me, cs, nb, p):
    return me + (1 - 2 * cs[p]) * (1 << (nb - 1 - p))


def at_dp(idx):
    return {"dp": idx}


def meet(n_dp, n_mp):
    nb, me, cs = coords(n_dp)
    m = lax.axis_index("mp")
    barrier = pltpu.get_barrier_semaphore()
    for p in range(nb):
        pl.semaphore_signal(
            barrier, inc=1, device_id=(flipped(me, cs, nb, p), m), device_id_type=pl.DeviceIdType.MESH
        )
    for j in range(1, n_mp):
        pl.semaphore_signal(
            barrier, inc=1, device_id=(me, lax.rem(m + j, n_mp)), device_id_type=pl.DeviceIdType.MESH
        )
    pl.semaphore_wait(barrier, nb + n_mp - 1)


def halves_order(nb):
    first = list(range(nb))
    second = list(range(nb))
    if nb > 1:
        second[0], second[1] = 1, 0
    return [first, second]


def gather_kernel(
    in_ref, sm_ref, rel_ref, tab_ref, reg_ref, sel_ref, selt_ref,
    out_ref, smo_ref, pos_ref, pen_ref,
    own_pos, own_sem, z_send, z_recv, st_send, st_recv, x_send, x_recv, *, n_dp, n_mp, wpos,
):
    nb, me, cs = coords(n_dp)
    m = lax.axis_index("mp")
    rows = in_ref.shape[0]
    orders = halves_order(nb)
    cut = [pl.ds(0, rows // 2), pl.ds(rows // 2, rows // 2)]
    meet(n_dp, n_mp)

    def slot(s, free=(), flip=None):
        idx = [slice(None) if p in free else (1 - cs[p] if p == flip else cs[p]) for p in range(nb)]
        return (s, *idx)

    own = pltpu.make_async_copy(in_ref, out_ref.at[slot(m)], own_sem)
    own.start()

    def z_copy(s, step, src):
        return pltpu.make_async_remote_copy(
            src_ref=src, dst_ref=out_ref.at[slot(s)], send_sem=z_send.at[s, (step + 1) // 2],
            recv_sem=z_recv.at[s], device_id=(me, m + step), device_id_type=pl.DeviceIdType.MESH,
        )

    def stage(s, half, t, mine=False, arriving=False):
        p = orders[half][t]
        region = slot(s, tuple(orders[half][:t]), p if arriving else None) + (cut[half],)
        src = in_ref.at[cut[half]] if mine else out_ref.at[region]
        return pltpu.make_async_remote_copy(
            src_ref=src, dst_ref=out_ref.at[region], send_sem=st_send.at[s, half, t],
            recv_sem=st_recv.at[s, half, t], device_id=(flipped(me, cs, nb, p), m),
            device_id_type=pl.DeviceIdType.MESH,
        )

    def guarded(ok, fn):
        if ok is None:
            fn()
        else:
            pl.when(ok)(fn)

    items = [[(m, 0, None)]]
    for k in range(1, n_mp):
        items.append([(m - k, 1, m - k >= 0), (m + k, -1, m + k < n_mp)])

    def forward(s, way, wait):
        for step in (1, -1) if way == 0 else (way,):
            edge = m < n_mp - 1 if step == 1 else m > 0

            def go(step=step):
                c = z_copy(s, step, in_ref if way == 0 else out_ref.at[slot(s)])
                c.wait_send() if wait else c.start()

            pl.when(edge)(go)

    def advance(s, way, t):
        if t == 0:
            if way != 0:
                z_copy(s, way, out_ref.at[slot(s)]).wait_recv()
            forward(s, way, False)
        for half in range(2):
            if t > 0:
                stage(s, half, t - 1, arriving=True).wait_recv()
            if t < nb:
                stage(s, half, t, mine=(t == 0 and way == 0)).start()

    def expand(t, total):
        return jnp.where(rel_ref[...] == t, tab_ref[pl.ds(t, 1), :], total)

    def x_copies(j):
        to = lax.rem(m + j, n_mp)
        pairs = ((sm_ref, smo_ref), (own_pos, pos_ref))
        return [
            pltpu.make_async_remote_copy(
                src_ref=src, dst_ref=dst.at[m], send_sem=x_send.at[k, j - 1],
                recv_sem=x_recv.at[k, j - 1], device_id=(me, to), device_id_type=pl.DeviceIdType.MESH,
            )
            for k, (src, dst) in enumerate(pairs)
        ]

    def x_arrivals(j):
        frm = lax.rem(m + n_mp - j, n_mp)
        pairs = ((sm_ref, smo_ref), (own_pos, pos_ref))
        return [
            pltpu.make_async_remote_copy(
                src_ref=src, dst_ref=dst.at[frm], send_sem=x_send.at[k, j - 1],
                recv_sem=x_recv.at[k, j - 1], device_id=(me, frm), device_id_type=pl.DeviceIdType.MESH,
            )
            for k, (src, dst) in enumerate(pairs)
        ]

    def small_work():
        own_pos[...] = lax.fori_loop(
            0, tab_ref.shape[0], expand, jnp.zeros(own_pos.shape, F32)
        )
        for j in range(1, n_mp):
            for c in x_copies(j):
                c.start()
        smo_ref[m] = sm_ref[...]
        pos_ref[m] = own_pos[...]
        by_key = dot(sel_ref[...], reg_ref[...], 1, 1)
        by_query = dot(reg_ref[...], selt_ref[...])
        cols = own_pos.shape[1]
        key = lax.broadcasted_iota(jnp.int32, own_pos.shape, 0)
        for w in range(pen_ref.shape[0]):
            same = by_key[w * WPAD : (w + 1) * WPAD, 0:1] == by_query[0:1, w * cols : (w + 1) * cols]
            pen_ref[w] = jnp.where(key < wpos, jnp.where(same, 0.0, -100.0), DEAD)

    for tick in range(n_mp + nb - 1):
        if tick == 1:
            small_work()
            own.wait()
        for t in reversed(range(nb)):
            k = tick - t
            if 0 <= k < n_mp:
                for s, way, ok in items[k]:
                    guarded(ok, functools.partial(advance, s, way, t))
    for group in items:
        for s, way, ok in group:
            guarded(ok, functools.partial(advance, s, way, nb))
    for j in range(1, n_mp):
        for c in x_arrivals(j):
            c.wait_recv()
        for c in x_copies(j):
            c.wait_send()
    for group in items:
        for s, way, ok in group:

            def finish(s=s, way=way):
                forward(s, way, True)
                for half in range(2):
                    for t in range(nb):
                        stage(s, half, t, mine=(t == 0 and way == 0)).wait_send()

            guarded(ok, finish)


def reduce_kernel(
    g_ref, rel_ref, tab_ref, qvs_ref, gb1_ref, gb2_ref, gin_ref, o_ref, so_ref, all_ref,
    t_rows, sm_ref, *rest, n_dp, n_mp, table_len, gh, gc,
):
    nb, me, cs = coords(n_dp)
    relay = Relay(gin_ref, all_ref, rest[-4:], n_mp, gin_ref.shape[0])
    rest = rest[:-4]
    m = lax.axis_index("mp")
    rows = g_ref.shape[-2]
    half_rows = rows // 2
    rest = list(rest)
    recv = [[rest.pop(0) for _ in range(nb)] for _ in range(2)]
    acc = [[rest.pop(0) for _ in range(nb)] for _ in range(2)]
    zin = [rest.pop(0) for _ in range(2)]
    s_in, s_acc, s_zin = rest.pop(0), rest.pop(0), rest.pop(0)
    send_sem, recv_sem, z_send, z_recv, s_send, s_recv, sz_send, sz_recv = rest
    orders = [list(reversed(o)) for o in halves_order(nb)]
    meet(n_dp, n_mp)

    def remote(src, dst, ssem, rsem, device):
        return pltpu.make_async_remote_copy(
            src_ref=src, dst_ref=dst, send_sem=ssem, recv_sem=rsem, device_id=device,
            device_id_type=pl.DeviceIdType.MESH,
        )

    def region(half, t, mine):
        left = sorted(set(range(nb)) - set(orders[half][:t]))
        p = orders[half][t]
        idx = [slice(None)] + [(cs[p] if mine else 1 - cs[p]) if q == p else slice(None) for q in left]
        if t == 0:
            idx.append(pl.ds(half * half_rows, half_rows))
        return tuple(idx)

    def source(half, t):
        return g_ref if t == 0 else acc[half][t - 1]

    def copy(half, t):
        p = orders[half][t]
        return remote(
            source(half, t).at[region(half, t, False)], recv[half][t], send_sem.at[half, t],
            recv_sem.at[half, t], (flipped(me, cs, nb, p), m),
        )

    def s_copy(t):
        src = sm_ref if t == 0 else s_acc.at[t - 1]
        return remote(src, s_in.at[t], s_send.at[t], s_recv.at[t], (flipped(me, cs, nb, t), m))

    def z_copy(half, j):
        to = lax.rem(m + j, n_mp)
        return remote(
            acc[half][nb - 1].at[to], zin[half].at[j - 1], z_send.at[half, j - 1],
            z_recv.at[half, j - 1], (me, to),
        )

    def sz_copy(j):
        to = lax.rem(m + j, n_mp)
        return remote(
            s_acc.at[nb - 1, to], s_zin.at[j - 1], sz_send.at[j - 1], sz_recv.at[j - 1], (me, to)
        )

    relay.start(greet=False)
    for half in range(2):
        copy(half, 0).start()

    t_rows[...] = jnp.zeros_like(t_rows)

    def pick(t, carry):
        hit = rel_ref[...] == t
        for g in range(n_mp):
            t_rows[g, pl.ds(t, 1), :] = col_sum(jnp.where(hit, tab_ref[g], 0.0))
        return carry

    lax.fori_loop(0, table_len, pick, 0)
    lane = lax.broadcasted_iota(jnp.int32, (t_rows.shape[1], 128), 1)
    width = gh * WPAD
    for g in range(n_mp):
        total = jnp.zeros(lane.shape, F32)
        for h in range(gh):
            part = jnp.sum(t_rows[g, :, h * WPAD : (h + 1) * WPAD], axis=1, keepdims=True)
            total = jnp.where(lane == h, part, total)
        sm_ref[g] = jnp.zeros_like(sm_ref[g])
        sm_ref[g, 0:8, :] = total.T[0:8, 0:width]
        cols = slice(g * gc, (g + 1) * gc)
        sm_ref[g, 8:9, :] = jnp.concatenate([qvs_ref[0:1, cols], qvs_ref[1:2, cols]], axis=1)
        hidden = gb1_ref[g] + gb2_ref[g]
        for k in range(hidden.shape[1] // width):
            sm_ref[g, 9 + k : 10 + k, :] = hidden[:, k * width : (k + 1) * width]
    s_copy(0).start()
    for t in range(nb):
        for half in range(2):
            copy(half, t).wait_recv()
            src = source(half, t)
            keep = region(half, t, True)
            deep = nb - 1 - t

            def add(s, carry, half=half, t=t, src=src, keep=keep, deep=deep):
                for k in range(1 << deep):
                    bits = [(k >> (deep - 1 - q)) & 1 for q in range(deep)]
                    inner = list(bits)
                    idx = [s] + [inner.pop(0) if isinstance(v, slice) else v for v in keep[1 : 1 + deep + 1]]
                    if t == 0:
                        idx.append(keep[-1])
                    mine = src[tuple(idx)].astype(F32)
                    other = recv[half][t][(s, *bits)].astype(F32)
                    acc[half][t][(s, *bits)] = (mine + other).astype(BF16)
                return carry

            lax.fori_loop(0, n_mp, add, 0)
            if t + 1 < nb:
                copy(half, t + 1).start()
            else:
                for j in range(1, n_mp):
                    z_copy(half, j).start()
        s_copy(t).wait_recv()
        before = sm_ref[...] if t == 0 else s_acc[t - 1]
        s_acc[t] = before + s_in[t]
        if t + 1 < nb:
            s_copy(t + 1).start()
        else:
            for j in range(1, n_mp):
                sz_copy(j).start()
        if t < n_mp - 1:
            relay.pass_on(t + 1)
    for k in range(nb + 1, n_mp):
        relay.pass_on(k)
    for half in range(2):
        total = acc[half][nb - 1][m].astype(F32)
        for j in range(1, n_mp):
            z_copy(half, j).wait_recv()
            total = total + zin[half][j - 1].astype(F32)
        o_ref[half * half_rows : (half + 1) * half_rows, :] = total
    s_total = s_acc[nb - 1, m]
    for j in range(1, n_mp):
        sz_copy(j).wait_recv()
        s_total = s_total + s_zin[j - 1]
    so_ref[...] = s_total
    for half in range(2):
        for t in range(nb):
            copy(half, t).wait_send()
        for j in range(1, n_mp):
            z_copy(half, j).wait_send()
    for t in range(nb):
        s_copy(t).wait_send()
    for j in range(1, n_mp):
        sz_copy(j).wait_send()
    relay.finish()


def unpack_kernel(
    red_ref, small_ref, gains_ref, offs_ref, qkv_ref, qv_ref, table_ref, proj_ref, fc1_ref, hb_ref, fc2_ref,
):
    gc = proj_ref.shape[1]
    hid = fc1_ref.shape[1]
    for kind in range(3):
        qkv_ref[kind] = red_ref[:, kind * gc : (kind + 1) * gc]
    at = 3 * gc
    proj_ref[...] = red_ref[:, at : at + gc]
    at += gc
    fc1_ref[...] = red_ref[:, at : at + hid]
    at += hid
    fc2_ref[...] = red_ref[:, at : at + hid]
    at += hid
    vec = red_ref[:, at : at + 128].T
    gains_ref[...] = vec[0:2]
    offs_ref[...] = vec[2:6]
    table_ref[...] = small_ref[0 : table_ref.shape[0], 0 : table_ref.shape[1]]
    qv_ref[0:1, :] = small_ref[8:9, 0:gc]
    qv_ref[1:2, :] = small_ref[8:9, gc : 2 * gc]
    for k in range(hid // (2 * gc)):
        hb_ref[:, k * 2 * gc : (k + 1) * 2 * gc] = small_ref[9 + k : 10 + k, :]


def gather_all(pack, small, rel, tab, reg, sel, selt, wpos, wins, n_dp, n_mp):
    nb = n_dp.bit_length() - 1
    rows, cols = pack.shape
    dma = pltpu.SemaphoreType.DMA
    shaped = jax.ShapeDtypeStruct
    vmem = pl.BlockSpec(memory_space=pltpu.VMEM)
    got, smalls, pos, pen = pl.pallas_call(
        functools.partial(gather_kernel, n_dp=n_dp, n_mp=n_mp, wpos=wpos),
        out_shape=(
            shaped((n_mp,) + (2,) * nb + (rows, cols), pack.dtype), shaped((n_mp,) + small.shape, F32),
            shaped((n_mp,) + rel.shape, F32), shaped((wins,) + rel.shape, F32),
        ),
        in_specs=[vmem] * 7,
        out_specs=[pl.BlockSpec(memory_space=pl.ANY), vmem, vmem, vmem],
        scratch_shapes=[
            pltpu.VMEM(rel.shape, F32),
            dma, dma((n_mp, 2)), dma((n_mp,)), dma((n_mp, 2, nb)), dma((n_mp, 2, nb)),
            dma((2, n_mp - 1)), dma((2, n_mp - 1)),
        ],
        compiler_params=pltpu.CompilerParams(collective_id=0, has_side_effects=True),
        name="gather_weights",
    )(pack, small, rel, tab, reg, sel, selt)
    return got.reshape(n_mp, n_dp * rows, cols), smalls, pos, pen


def reduce_all(grads, rel, tab, qvs, gb1, gb2, gin, n_dp, n_mp, table_len, gh, gc):
    nb = n_dp.bit_length() - 1
    _, d, cols = grads.shape
    rows = d // n_dp
    half = rows // 2
    dma = pltpu.SemaphoreType.DMA
    parts = [pltpu.VMEM((n_mp,) + (2,) * (nb - 1 - t) + (half, cols), BF16) for t in range(nb)]
    sr, sc = 16, gh * WPAD
    assert sc == 2 * gc and 9 + gb1.shape[2] // sc <= sr and table_len <= sc
    return pl.pallas_call(
        functools.partial(
            reduce_kernel, n_dp=n_dp, n_mp=n_mp, table_len=table_len, gh=gh, gc=gc
        ),
        out_shape=(
            jax.ShapeDtypeStruct((rows, cols), F32), jax.ShapeDtypeStruct((sr, sc), F32),
            jax.ShapeDtypeStruct((n_mp,) + gin.shape, BF16),
        ),
        in_specs=[pl.BlockSpec(memory_space=pltpu.VMEM)] * 7,
        out_specs=[pl.BlockSpec(memory_space=pltpu.VMEM)] * 2 + [pl.BlockSpec(memory_space=pl.ANY)],
        scratch_shapes=[pltpu.VMEM((n_mp, sc, sc), F32), pltpu.VMEM((n_mp, sr, sc), F32)]
        + parts * 4
        + [pltpu.VMEM((n_mp - 1, half, cols), BF16)] * 2
        + [pltpu.VMEM((nb, n_mp, sr, sc), F32)] * 2
        + [pltpu.VMEM((n_mp - 1, sr, sc), F32)]
        + [dma((2, nb))] * 2 + [dma((2, n_mp - 1))] * 2 + [dma((nb,))] * 2 + [dma((n_mp - 1,))] * 2
        + Relay.scratch(gin.shape[0], n_mp),
        compiler_params=pltpu.CompilerParams(
            collective_id=1, has_side_effects=True, vmem_limit_bytes=60 * 1024 * 1024
        ),
        name="reduce_gradients",
    )(grads.reshape((n_mp,) + (2,) * nb + (rows, cols)), rel, tab, qvs, gb1, gb2, gin)


def whole(shape):
    zero = (0,) * len(shape)
    return pl.BlockSpec(shape, lambda i: zero, pipeline_mode=pl.Buffered(1))


def shards(
    block_input, out_grad, norm_gains, offsets, qkv_weight, qv_bias, pos_table,
    proj_weight, fc1_weight, fc1_bias, fc2_weight, rel_index, region_ids, *, n_dp, n_mp,
):
    images, tokens, d = block_input.shape
    groups = n_mp
    gh, table_len = pos_table.shape
    gc = gh * HD
    hid = fc1_bias.shape[0]
    heads = groups * gh
    rows_w = qkv_weight.shape[0]
    wpos = rel_index.shape[0]
    wins = tokens // wpos
    prow = wins * WPAD
    trow = -(-tokens // 16) * 16
    mine = images // n_mp
    imgs = 2 if mine % 2 == 0 else 1
    steps = mine // imgs
    m = lax.axis_index("mp")

    n_vec = norm_gains.shape[1] + offsets.shape[1]
    pack = jnp.concatenate(
        [
            proj_weight, fc1_weight, fc2_weight, qkv_weight.reshape(rows_w, 3 * gc), norm_gains,
            offsets, jnp.zeros((rows_w, 128 - n_vec), BF16),
        ],
        axis=1,
    )
    qkv_at = (gc + 2 * hid) // (3 * gc)
    vec_at = (4 * gc + 2 * hid) // 128
    assert qkv_at * 3 * gc == gc + 2 * hid and gc == 128
    small = jnp.concatenate([qv_bias.reshape(-1), fc1_bias]).astype(F32).reshape(-1, 128)
    small = jnp.pad(small, ((0, -small.shape[0] % 8), (0, 0)))
    pad_w = WPAD - wpos
    rel_t = jnp.pad(rel_index.T, ((0, pad_w), (0, pad_w)), constant_values=-1)
    rel = jnp.tile(rel_t, (1, gh))
    tab = jnp.repeat(pos_table.T, WPAD, axis=1)
    reg = jnp.broadcast_to(region_ids.reshape(1, -1), (8, tokens)).astype(BF16)
    plain = pick_matrix(tokens, 0)
    selt = np.tile(plain.T.reshape(tokens, wins, 1, WPAD), (1, 1, gh, 1)).reshape(tokens, -1)
    got, smalls_in, pos, pen = gather_all(
        pack, small, rel, tab, reg, jnp.asarray(plain, BF16), jnp.asarray(selt, BF16), wpos, wins,
        n_dp, n_mp,
    )

    pick = pick_matrix(tokens)
    pick_pad = np.pad(pick, ((0, 0), (0, trow - tokens)))
    pm = jnp.asarray(pick, BF16)
    pmp = jnp.asarray(pick_pad, BF16)
    pmt = jnp.asarray(pick_pad.T, BF16)
    full = groups * gc
    x_mine = lax.dynamic_slice_in_dim(block_input, m * mine, mine, 0)
    gy_mine = lax.dynamic_slice_in_dim(out_grad, m * mine, mine, 0)
    rows = imgs * trow
    prows = imgs * prow
    wa_spec = pl.BlockSpec((groups, d, 3 * gc), lambda i: (0, 0, qkv_at), pipeline_mode=pl.Buffered(1))
    wb_spec = pl.BlockSpec((groups, d, gc + 2 * hid), lambda i: (0, 0, 0), pipeline_mode=pl.Buffered(1))
    wp_spec = pl.BlockSpec((groups, d, gc), lambda i: (0, 0, 0), pipeline_mode=pl.Buffered(1))
    any_spec = pl.BlockSpec(memory_space=pl.ANY)

    def part_spec(shape, c):
        tail = (0,) * (len(shape) - 1)
        return pl.BlockSpec(shape, lambda i, c=c: (c + i, *tail))

    vec_spec = pl.BlockSpec((1, d, 128), lambda i: (0, 0, vec_at), pipeline_mode=pl.Buffered(1))
    shaped = jax.ShapeDtypeStruct
    names = dict(
        imgs=imgs, groups=groups, gh=gh, gc=gc, hid=hid, prow=prow, trow=trow, tokens=tokens, n_mp=n_mp
    )
    big = (
        shaped((mine * prow, 3 * full), BF16), shaped((mine * prow, d), BF16),
        shaped((mine * wins, groups, WPAD, gh * WPAD), F32), shaped((mine * trow, full), BF16),
    )
    big_fed = (
        shaped((mine * trow, d), F32), shaped((mine * trow, groups * hid), BF16),
        shaped((mine * trow, groups * hid), BF16), shaped((mine * trow, d), BF16),
        shaped((mine * trow, d), BF16),
    )
    probs_block = (imgs * wins, groups, WPAD, gh * WPAD)
    sent, kept, ghbs, sums_bs, arrived = [], [], [], [], []
    first = 0
    for count in (1, steps - 1):
        c = first
        first += count
        relayed = len(sent) > 0
        got_back = pl.pallas_call(
            functools.partial(forward_kernel, kept=len(kept), relayed=relayed, **names),
            out_shape=big + (shaped((count, imgs, tokens, d), BF16),) + big_fed
            + (shaped((groups, 1, hid), F32), shaped((8, d), F32))
            + ((shaped((n_mp,) + sent[0].shape, BF16),) if relayed else ()),
            grid=(count,),
            in_specs=[
                part_spec((imgs, tokens, d), c), part_spec((imgs, tokens, d), c), wa_spec, wb_spec,
                vec_spec, whole(smalls_in.shape), whole(pos.shape), whole(pen.shape), whole(pm.shape),
                whole(pmt.shape),
            ] + [any_spec] * len(kept) + ([whole(sent[0].shape)] if relayed else []),
            out_specs=[
                part_spec((prows, 3 * full), c), part_spec((prows, d), c), part_spec(probs_block, c),
                part_spec((rows, full), c),
                pl.BlockSpec((None, imgs, tokens, d), lambda i: (i, 0, 0, 0)),
                part_spec((rows, d), c), part_spec((rows, groups * hid), c),
                part_spec((rows, groups * hid), c), part_spec((rows, d), c), part_spec((rows, d), c),
                whole((groups, 1, hid)), whole((8, d)),
            ] + ([any_spec] if relayed else []),
            scratch_shapes=[pltpu.VMEM((prows, full), BF16)] + [pltpu.VMEM((rows, d), F32)] * 4
            + (Relay.scratch(sent[0].shape[0], n_mp) if relayed else []),
            input_output_aliases={10 + k: k if k < 4 else k + 1 for k in range(len(kept))},
            compiler_params=pltpu.CompilerParams(
                vmem_limit_bytes=60 * 1024 * 1024,
                **(dict(collective_id=2, has_side_effects=True) if relayed else {}),
            ),
            name="forward",
        )(x_mine, gy_mine, got, got, got, smalls_in, pos, pen, pm, pmt, *kept, *sent)
        kept = list(got_back[0:4]) + list(got_back[5:10])
        sent = [got_back[4]]
        ghbs.append(got_back[10])
        sums_bs.append(got_back[11])
        arrived += got_back[12:]
    qkv, hw, probs, attn, gx1, act, gpb, h2, gyp = kept
    gcols = 4 * gc + 2 * hid + 128

    def early(shape):
        tail = (0,) * (len(shape) - 1)
        return pl.BlockSpec(shape, lambda i: (jnp.minimum(i, steps - 1), *tail))

    def late(r, c):
        return pl.BlockSpec((r, c), lambda i: (0, jnp.maximum(i - steps, 0)))

    trows_all, prows_all = mine * trow, mine * prow
    gin, gtab, gqv, gw, out_2 = pl.pallas_call(
        functools.partial(backward_kernel, steps=steps, **names),
        out_shape=(
            shaped((mine, tokens, d), BF16), shaped((groups, WPAD, gh * WPAD), F32),
            shaped((8, full), F32), shaped((groups, d, gcols), BF16),
            shaped((n_mp,) + sent[0].shape, BF16),
        ),
        grid=(steps + groups,),
        in_specs=[
            early((imgs, tokens, d)), early((rows, d)), early((prows, 3 * full)), early(probs_block),
            wa_spec, wp_spec, vec_spec, whole(pmp.shape), whole(pmt.shape), whole(hw.shape),
            whole(gx1.shape), late(trows_all, gc), whole(h2.shape), late(trows_all, hid),
            whole(gyp.shape), late(trows_all, hid), whole((8, d)), whole((8, d)), any_spec,
        ],
        out_specs=[
            early((imgs, tokens, d)), whole((groups, WPAD, gh * WPAD)), whole((8, full)),
            pl.BlockSpec((1, d, gcols), lambda i: (jnp.maximum(i - steps, 0), 0, 0)), any_spec,
        ],
        scratch_shapes=[
            pltpu.VMEM((3, prows_all, full), BF16), pltpu.VMEM((8, d), F32),
            pltpu.VMEM((prows, d), BF16), pltpu.VMEM((prows, full), BF16), pltpu.VMEM((128, d), F32),
            pltpu.VMEM((d, prows_all), BF16), pltpu.VMEM((d, trows_all), BF16),
            pltpu.VMEM((d, trows_all), BF16), pltpu.VMEM((d, trows_all), BF16),
        ] + Relay.scratch(sent[0].shape[0], n_mp),
        compiler_params=pltpu.CompilerParams(
            vmem_limit_bytes=60 * 1024 * 1024, collective_id=3, has_side_effects=True
        ),
        name="backward",
    )(
        x_mine, gx1, qkv, probs, got, got, got, pmp, pmt, hw, gx1, attn, h2, gpb, gyp, act, *sums_bs,
        *sent,
    )
    arrived.append(out_2)
    red, red_s, input_grad = reduce_all(
        gw, rel, gtab, gqv, *ghbs, gin.reshape(steps, imgs, tokens, d), n_dp, n_mp, table_len, gh, gc
    )
    input_grad = input_grad.reshape(images, tokens, d)
    out_parts = arrived
    block_output = jnp.concatenate(out_parts, axis=1).reshape(images, tokens, d)
    gains_t, offs_t, qkv_t, qv_grad, table_grad, proj_grad, fc1_grad, hb_grad, fc2_grad = pl.pallas_call(
        unpack_kernel,
        out_shape=tuple(
            shaped(shape, F32)
            for shape in (
                (2, rows_w), (4, rows_w), (3, rows_w, gc), (2, gc), (gh, table_len), (rows_w, gc),
                (rows_w, hid), (1, hid), (rows_w, hid),
            )
        ),
        name="unpack",
    )(red, red_s)
    return (
        block_output, input_grad, gains_t.T, offs_t.T, qkv_t.transpose(1, 0, 2), qv_grad, table_grad,
        proj_grad, fc1_grad, hb_grad.reshape(hid), fc2_grad,
    )


def solution(mesh):
    in_specs = (
        P("dp", None, None), P("dp", None, None), P("dp", None), P("dp", None), P("dp", None, "mp"),
        P(None, "mp"), P("mp", None), P("dp", "mp"), P("dp", "mp"), P("mp"), P("dp", "mp"), P(), P(),
    )
    out_specs = (
        P("dp", None, None), P("dp", None, None), P("dp", None), P("dp", None), P("dp", None, "mp"),
        P(None, "mp"), P("mp", None), P("dp", "mp"), P("dp", "mp"), P("mp"), P("dp", "mp"),
    )
    body = functools.partial(shards, n_dp=mesh.shape["dp"], n_mp=mesh.shape["mp"])
    return jax.shard_map(body, mesh=mesh, in_specs=in_specs, out_specs=out_specs, check_vma=False)
```

time: 507 us -> 306 us (0.60)
  waiting for transfers between devices: 266 us -> 0 us
  Pallas kernels: 99.7 us -> 276 us
  blocking collectives: 72.5 us -> 0 us
  local copies, waits for them, and re-layouts: 44.2 us -> 24 us
  between operations: 14.4 us -> 0.94 us
    pallas_call x3 -> x6, Pallas kernels: 99.7 us -> 276 us  [the longest x1 101 us: reduce_all(): pl.pallas_call(functools.partial(reduce_kernel, n_dp=n_dp, n_mp=n_mp, tab...]
    all_gather x4 -> x0, waiting for transfers between devices: 156 us -> none  [the longest x1 86.3 us: shards(): block_output = lax.all_gather(out, 'mp', axis=0, tiled=True)]
    reduce_scatter x4 -> x0, waiting for transfers between devices: 108 us -> none  [the longest x2 91.5 us: scatter(): part = lax.psum_scatter(g, 'dp', scatter_dimension=1, tiled=True)]
    psum x1 -> x0, blocking collectives: 39.6 us -> none  [shards(): smalls = lax.psum(smalls, ('dp', 'mp'))]
    all_gather x2 -> x0, blocking collectives: 32.8 us -> none  [gather(): lax.all_gather(pack, 'mp', axis=0, tiled=False)]
    unnamed x30 -> x13, local copies, waits for them, and re-layouts: 27 us -> 15.4 us
  transfers between devices with their start and end apart: 8 -> 0, of which waited for: 6 -> 0; matrix products, arithmetic and copies ran while one was open for 9% -> 0% of each run, Pallas kernels for 5% -> 0%
where the time goes in v2:
time: 306 us
  Pallas kernels  276 us (90%)
  local copies, waits for them, and re-layouts  24 us (8%)
  other arithmetic  4.37 us (1%)
    pallas_call x1, Pallas kernels, reduce_all(): pl.pallas_call(functools.partial(reduce_kernel, n_dp=n_dp, n_mp=n_mp, tab...  101 us
    pallas_call x1, Pallas kernels, shards(): pl.pallas_call(functools.partial(backward_kernel, steps=steps, **names),...  73 us
    pallas_call x2, Pallas kernels, shards(): pl.pallas_call(functools.partial(forward_kernel, kept=len(kept), relayed=...  57.1 us
    pallas_call x1, Pallas kernels, gather_all(): pl.pallas_call(functools.partial(gather_kernel, n_dp=n_dp, n_mp=n_mp, wpo...  43.8 us
    unnamed x13, local copies, waits for them, and re-layouts  15.4 us

profile of v2, /device:TPU:0, one launch (start us, length us, event | category | flops | bytes accessed | tf_op | source)
XLA Modules:
  0.0 305.7 jit_solution(12513588416539627242)
XLA Ops:
  0.6 0.0 copy-start
  0.7 0.7 maximum_bitcast_fusion
  1.4 0.6 pad_convert_fusion.sm_ref
  2.0 0.7 convert_element_type.13
  2.7 0.1 convert_element_type.14
  2.8 0.6 broadcast_in_dim.13.reg_ref
  3.4 0.8 copy.50
  4.1 0.8 copy.51
  4.9 0.8 copy.58
  5.8 0.0 copy-done
  5.8 0.8 tile.10.rel_ref
  6.6 1.6 concatenate.9.in_ref
  8.2 0.7 broadcast_in_dim.12
  8.9 0.8 copy.53.tab_ref
  9.7 3.9 %constant_dynamic-slice_fusion = (bf16[6,196,512]{2,0,1:T(8,128)(2,1)S(1)}, bf16[6,196,512]{2,0,1:T(8,128)(2,1)S(1)}) fusion(bf16[24,196,512]{2,0,1:T(8,128)(2,1)} %param.19, s32[]{:T(128)S(6)} %select_n.4, bf16[24,196,512]{2,0,1:T(8,128)(2,1)} %param.18), kind=kLoop, calls=%fused_computation.4 | loop fusion | bytes 4816900 | tf_op jit(solution)/shard_map/dynamic_slice | solution.py:910
  13.7 1.4 copy.57.refs_1_
  15.1 1.4 copy.56.refs_0_
  16.5 43.8 %gather_weights.1 = (bf16[4,2,2,2,64,1664]{5,4,3,2,1,0:T(8,128)(2,1)}, f32[4,8,128]{2,1,0:T(8,128)}, f32[4,64,256]{2,1,0:T(8,128)}, f32[4,64,256]{2,1,0:T(8,128)}) custom-call(bf16[64,1664]{1,0:T(8,128)(2,1)} %concatenate.9.in_ref, f32[8,128]{1,0:T(8,128)} %pad_convert_fusion.sm_ref, s32[64,256]{1,0:T(8,128)} %tile.10.rel_ref, f32[169,256]{1,0:T(8,128)} %copy.53.tab_ref, ...), custom_call_target="tpu_custom_call" | custom-call | tf_op jit(solution)/shard_map/gather_weights/pallas_call | solution.py:801
  60.2 18.4 %forward.2 = (bf16[1536,1536]{1,0:T(8,128)(2,1)}, bf16[1536,512]{1,0:T(8,128)(2,1)}, f32[24,4,64,256]{3,2,1,0:T(8,128)}, bf16[1248,512]{1,0:T(8,128)(2,1)}, bf16...) custom-call(bf16[6,196,512]{2,1,0:T(8,128)(2,1)} %copy.56.refs_0_, ...), custom_call_target="tpu_custom_call" | custom-call | tf_op jit(solution)/shard_map/forward/pallas_call | solution.py:943
  78.6 38.7 %forward.3 = (bf16[1536,1536]{1,0:T(8,128)(2,1)}, bf16[1536,512]{1,0:T(8,128)(2,1)}, f32[24,4,64,256]{3,2,1,0:T(8,128)}, bf16[1248,512]{1,0:T(8,128)(2,1)}, bf16...) custom-call(bf16[6,196,512]{2,1,0:T(8,128)(2,1)} %copy.56.refs_0_, ...), custom_call_target="tpu_custom_call", output_to_operand_aliasing={{0}: (10, {}), {1}: (11, {}), {2}: (12, {}), {3}: (13, {}),... | custom-call | tf_op jit(solution)/shard_map/forward/pallas_call | solution.py:943
  117.3 0.0 copy-start.2
  117.4 73.0 %backward.1 = (bf16[6,196,512]{2,1,0:T(8,128)(2,1)}, f32[4,64,256]{2,1,0:T(8,128)}, f32[8,512]{1,0:T(8,128)}, bf16[4,512,1664]{2,1,0:T(8,128)(2,1)}, bf16[4,2,2,196,512]{4,3,2,1,0:T(8,128)(2,1)}) custom-call(bf16[6,196,512]{2,1,0:T(8,128)(2,1)} %copy.56.refs_0_, f32[1248,512]{1,0:T(8,128)} %get-tuple-element.72.refs_1_.refs_10_, ...), custom_call_target="tpu_custom_call" | custom-call | tf_op jit(solution)/shard_map/backward/pallas_call | solution.py:987
  190.3 0.0 copy-done.2
  190.4 2.4 pad_maximum_fusion
  192.7 4.0 %copy.54 = bf16[24,196,512]{2,0,1:T(8,128)(2,1)} copy(bf16[24,196,512]{2,1,0:T(8,128)(2,1)S(1)} %bitcast.29) | data formatting | bytes 9633792
  196.7 100.7 %reduce_gradients.1 = (f32[64,1664]{1,0:T(8,128)}, f32[16,256]{1,0:T(8,128)}, bf16[4,3,2,196,512]{4,3,2,1,0:T(8,128)(2,1)}) custom-call(bf16[4,2,2,2,64,1664]{5,4,3,2,1,0:T(8,128)(2,1)} %bitcast.30, s32[64,256]{1,0:T(8,128)} %tile.10.rel_ref, f32[4,64,256]{2,1,0:T(8,128)} %get-tuple-element.86.tab_ref, f32[8,512]{1,0:T(8,128)} %get-tuple-element.87.qvs_ref, ...), custom_call_target="tpu_custom_call" | custom-call | tf_op jit(solution)/shard_map/reduce_gradients/pallas_call | solution.py:829
  297.4 0.0 copy-start.1
  297.4 6.3 %copy.55 = bf16[24,196,512]{2,0,1:T(8,128)(2,1)} copy(bf16[24,196,512]{2,1,0:T(8,128)(2,1)} %bitcast.31) | data formatting | bytes 9633792
  303.7 1.8 unpack.1
  305.5 0.0 copy-done.1
  (4 shorter events, 0.0 us)
Async XLA Ops:
  0.6 5.1 %copy-start = (bf16[64,3,128]{2,0,1:T(8,128)(2,1)S(1)}, bf16[64,3,128]{2,0,1:T(8,128)(2,1)}, u32[]{:S(2)}) copy-start(bf16[64,3,128]{2,0,1:T(8,128)(2,1)} %param.22) | copy-start | bytes 147460
  117.3 73.0 %copy-start.2 = (bf16[4,1,2,196,512]{4,3,2,1,0:T(8,128)(2,1)S(1)}, bf16[4,1,2,196,512]{4,3,2,1,0:T(8,128)(2,1)}, u32[]{:S(2)}) copy-start(bf16[4,1,2,196,512]{4,3,2,1,0:T(8,128)(2,1)} %get-tuple-element.71) | copy-start | bytes 4816900
  297.4 8.1 %copy-start.1 = (bf16[64,3,128]{2,0,1:T(8,128)(2,1)S(1)}, bf16[64,3,128]{2,0,1:T(8,128)(2,1)}, u32[]{:S(2)}) copy-start(bf16[64,3,128]{2,0,1:T(8,128)(2,1)} %param.22) | copy-start | bytes 147460

commit v3 on v2

--- a/solution.py
+++ b/solution.py
@@ -144,7 +144,7 @@
 
 def feed_kernel(
     x_ref, gy_ref, attn_ref, w_ref, vec_ref, sm_ref,
-    *rest, imgs, groups, gc, hid, trow, tokens,
+    *rest, imgs, groups, gc, hid, trow, tokens, middle,
 ):
     out_ref, gx1_ref, act_ref, gpb_ref, h2_ref, gyp_ref, gb_ref, sums_ref, xs, gys, mlp, gh2 = rest[-12:]
     vec = vectors(vec_ref)
@@ -169,6 +169,8 @@
     gh2[...] = jnp.zeros_like(gh2)
 
     for g in range(groups):
+        if g == groups // 2:
+            middle()
         fc1 = w_ref[g, :, gc : gc + hid]
         fc2 = w_ref[g, :, gc + hid : gc + 2 * hid]
         pre = dot(h2_ref[...], fc1) + jnp.concatenate(
@@ -359,7 +361,17 @@
     attw, xs, gys, mlp, gh2 = refs[:5]
     step = pl.program_id(0)
     last = pl.num_programs(0) - 1
-    relay = Relay(source, target, refs[5:], n_mp, 0) if relayed else None
+    relay = Relay(source, target, refs[5:], n_mp, source.shape[0]) if relayed else None
+    hooks = {(0, 1): (1, 0), (0, 2): (1, 1), (0, 3): (2, 0), (1, 1): (2, 1)}
+    if relayed and (n_mp != 4 or relay.pieces != 2):
+        hooks = {}
+    done = [pair for pair in hooks.values()]
+
+    def place(at):
+        for (j, here), pair in hooks.items():
+            if relayed and here == at:
+                pl.when(step == j)(lambda pair=pair: relay.pass_one(*pair))
+
 
     if relayed:
         pl.when(step == 0)(relay.start)
@@ -367,12 +379,22 @@
         x, wa, vec, sm, pos, pen, pm, pmt, qkv, hw, probs, attn, attw,
         imgs=imgs, groups=groups, gh=gh, prow=prow, trow=trow,
     )
+    place(1)
     feed_kernel(
         x, gy, attn, wb, vec, sm, out, gx1, act, gpb, h2, gyp, gb, sums, xs, gys, mlp, gh2,
-        imgs=imgs, groups=groups, gc=gc, hid=hid, trow=trow, tokens=tokens,
-    )
+        imgs=imgs, groups=groups, gc=gc, hid=hid, trow=trow, tokens=tokens, middle=lambda: place(2),
+    )
+    place(3)
     if relayed:
-        pl.when(step == last)(relay.finish)
+
+        def finish():
+            for k in range(1, n_mp):
+                for p in range(relay.pieces):
+                    if (k, p) not in done:
+                        relay.pass_one(k, p)
+            relay.finish()
+
+        pl.when(step == last)(finish)
 
 
 def backward_kernel(*refs, imgs, steps, groups, gh, gc, hid, prow, trow, tokens, n_mp):
@@ -387,14 +409,16 @@
     def hook(at):
         return lambda: relay.pass_one(*todo[at])
 
-    placed = max(0, min(2 * steps - 1, len(todo) - relay.pieces))
+    step = pl.program_id(0)
+    in_steps = {1: 1, 2: 2}
+    at_ends = {0: 0, 3: 3}
+    placed = 4
+    if steps < 3 or relay.pieces != 2 or n_mp != 4:
+        in_steps, at_ends, placed = {}, {}, 0
 
     def middle():
-        for j in range(1, steps):
-            if 2 * j - 1 < placed:
-                pl.when(step == j)(hook(2 * j - 1))
-
-    step = pl.program_id(0)
+        for j, at in in_steps.items():
+            pl.when(step == j)(hook(at))
 
     @pl.when(step == 0)
     def _():
@@ -407,9 +431,12 @@
             imgs=imgs, groups=groups, gh=gh, prow=prow, trow=trow, tokens=tokens, middle=middle,
         )
 
-    for j in range(steps):
-        if 2 * j < placed:
-            pl.when(step == j)(hook(2 * j))
+    def end_hooks(steps_here):
+        for j, at in at_ends.items():
+            if j in steps_here:
+                pl.when(step == j)(hook(at))
+
+    end_hooks(range(steps))
 
     @pl.when(step >= steps)
     def _():
@@ -439,6 +466,8 @@
         at += hid
         gw[0, :, at : at + vsum.shape[0]] = vsum[...].T.astype(BF16)
 
+    end_hooks(range(steps, steps + groups))
+
     @pl.when(step == steps + groups - 1)
     def _():
         for k, p in todo[placed:]:
@@ -484,9 +513,9 @@
 
 
 def gather_kernel(
-    in_ref, sm_ref, rel_ref, tab_ref, reg_ref, sel_ref, selt_ref,
-    out_ref, smo_ref, pos_ref, pen_ref,
-    own_pos, own_sem, z_send, z_recv, st_send, st_recv, x_send, x_recv, *, n_dp, n_mp, wpos,
+    in_ref, sm_ref, rel_in, tab_in, reg_ref, row_ref, col_ref,
+    out_ref, smo_ref, pos_ref, pen_ref, rel_ref,
+    own_pos, rel_pad, tab_pad, tab_ref, own_sem, z_send, z_recv, st_send, st_recv, x_send, x_recv, *, n_dp, n_mp, wpos,
 ):
     nb, me, cs = coords(n_dp)
     m = lax.axis_index("mp")
@@ -575,20 +604,32 @@
         ]
 
     def small_work():
+        gh = tab_in.shape[0]
+        rel_pad[...] = jnp.full(rel_pad.shape, -1.0, F32)
+        rel_pad[0:wpos, 0:wpos] = rel_in[...].astype(F32)
+        rel_t = rel_pad[...].T[0:WPAD, 0:WPAD]
+        rel_ref[...] = jnp.concatenate([rel_t] * gh, axis=1).astype(jnp.int32)
+        tab_pad[...] = jnp.zeros_like(tab_pad)
+        tab_pad[0:gh, 0 : tab_in.shape[1]] = tab_in[...]
+        tab_t = tab_pad[...].T
+        tab_ref[...] = jnp.concatenate(
+            [jnp.broadcast_to(tab_t[:, h : h + 1], (tab_t.shape[0], WPAD)) for h in range(gh)], axis=1
+        )
         own_pos[...] = lax.fori_loop(
-            0, tab_ref.shape[0], expand, jnp.zeros(own_pos.shape, F32)
+            0, tab_in.shape[1], expand, jnp.zeros(own_pos.shape, F32)
         )
         for j in range(1, n_mp):
             for c in x_copies(j):
                 c.start()
         smo_ref[m] = sm_ref[...]
         pos_ref[m] = own_pos[...]
-        by_key = dot(sel_ref[...], reg_ref[...], 1, 1)
-        by_query = dot(reg_ref[...], selt_ref[...])
-        cols = own_pos.shape[1]
+        picked = dot(row_ref[...], reg_ref[...].astype(F32).astype(BF16))
+        by_key = jnp.sum(picked * col_ref[...], axis=1, keepdims=True)
+        by_query = jnp.broadcast_to(by_key, (by_key.shape[0], 128)).T
         key = lax.broadcasted_iota(jnp.int32, own_pos.shape, 0)
         for w in range(pen_ref.shape[0]):
-            same = by_key[w * WPAD : (w + 1) * WPAD, 0:1] == by_query[0:1, w * cols : (w + 1) * cols]
+            here = slice(w * WPAD, (w + 1) * WPAD)
+            same = by_key[here] == jnp.concatenate([by_query[0:1, here]] * gh, axis=1)
             pen_ref[w] = jnp.where(key < wpos, jnp.where(same, 0.0, -100.0), DEAD)
 
     for tick in range(n_mp + nb - 1):
@@ -792,29 +833,32 @@
         hb_ref[:, k * 2 * gc : (k + 1) * 2 * gc] = small_ref[9 + k : 10 + k, :]
 
 
-def gather_all(pack, small, rel, tab, reg, sel, selt, wpos, wins, n_dp, n_mp):
+def gather_all(pack, small, rel, tab, reg, row, col, wpos, wins, n_dp, n_mp):
     nb = n_dp.bit_length() - 1
     rows, cols = pack.shape
     dma = pltpu.SemaphoreType.DMA
     shaped = jax.ShapeDtypeStruct
     vmem = pl.BlockSpec(memory_space=pltpu.VMEM)
-    got, smalls, pos, pen = pl.pallas_call(
+    wide = (WPAD, tab.shape[0] * WPAD)
+    assert tab.shape[1] <= 256 and tab.shape[0] <= 128
+    got, smalls, pos, pen, rel_t = pl.pallas_call(
         functools.partial(gather_kernel, n_dp=n_dp, n_mp=n_mp, wpos=wpos),
         out_shape=(
             shaped((n_mp,) + (2,) * nb + (rows, cols), pack.dtype), shaped((n_mp,) + small.shape, F32),
-            shaped((n_mp,) + rel.shape, F32), shaped((wins,) + rel.shape, F32),
+            shaped((n_mp,) + wide, F32), shaped((wins,) + wide, F32), shaped(wide, jnp.int32),
         ),
         in_specs=[vmem] * 7,
-        out_specs=[pl.BlockSpec(memory_space=pl.ANY), vmem, vmem, vmem],
+        out_specs=[pl.BlockSpec(memory_space=pl.ANY), vmem, vmem, vmem, vmem],
         scratch_shapes=[
-            pltpu.VMEM(rel.shape, F32),
+            pltpu.VMEM(wide, F32), pltpu.VMEM((128, 128), F32), pltpu.VMEM((128, 256), F32),
+            pltpu.VMEM((256, wide[1]), F32),
             dma, dma((n_mp, 2)), dma((n_mp,)), dma((n_mp, 2, nb)), dma((n_mp, 2, nb)),
             dma((2, n_mp - 1)), dma((2, n_mp - 1)),
         ],
         compiler_params=pltpu.CompilerParams(collective_id=0, has_side_effects=True),
         name="gather_weights",
-    )(pack, small, rel, tab, reg, sel, selt)
-    return got.reshape(n_mp, n_dp * rows, cols), smalls, pos, pen
+    )(pack, small, rel, tab, reg, row, col)
+    return got.reshape(n_mp, n_dp * rows, cols), smalls, pos, pen, rel_t
 
 
 def reduce_all(grads, rel, tab, qvs, gb1, gb2, gin, n_dp, n_mp, table_len, gh, gc):
@@ -888,16 +932,14 @@
     assert qkv_at * 3 * gc == gc + 2 * hid and gc == 128
     small = jnp.concatenate([qv_bias.reshape(-1), fc1_bias]).astype(F32).reshape(-1, 128)
     small = jnp.pad(small, ((0, -small.shape[0] % 8), (0, 0)))
-    pad_w = WPAD - wpos
-    rel_t = jnp.pad(rel_index.T, ((0, pad_w), (0, pad_w)), constant_values=-1)
-    rel = jnp.tile(rel_t, (1, gh))
-    tab = jnp.repeat(pos_table.T, WPAD, axis=1)
-    reg = jnp.broadcast_to(region_ids.reshape(1, -1), (8, tokens)).astype(BF16)
-    plain = pick_matrix(tokens, 0)
-    selt = np.tile(plain.T.reshape(tokens, wins, 1, WPAD), (1, 1, gh, 1)).reshape(tokens, -1)
-    got, smalls_in, pos, pen = gather_all(
-        pack, small, rel, tab, reg, jnp.asarray(plain, BF16), jnp.asarray(selt, BF16), wpos, wins,
-        n_dp, n_mp,
+    plain = padded_order(0)
+    cells = np.arange(SIDE)[None, :]
+    real = plain[:, None] >= 0
+    row = (real & (plain[:, None] // SIDE == cells)).astype(np.float32)
+    col = (real & (plain[:, None] % SIDE == cells)).astype(np.float32)
+    got, smalls_in, pos, pen, rel = gather_all(
+        pack, small, rel_index, pos_table, region_ids, jnp.asarray(row, BF16), jnp.asarray(col, F32),
+        wpos, wins, n_dp, n_mp,
     )
 
     pick = pick_matrix(tokens)
@@ -970,9 +1012,11 @@
         )(x_mine, gy_mine, got, got, got, smalls_in, pos, pen, pm, pmt, *kept, *sent)
         kept = list(got_back[0:4]) + list(got_back[5:10])
         sent = [got_back[4]]
+        if not relayed:
+            sent = [sent[0].reshape(count * imgs, 1, tokens, d)]
         ghbs.append(got_back[10])
         sums_bs.append(got_back[11])
-        arrived += got_back[12:]
+        arrived += [v.reshape(n_mp, -1, imgs, tokens, d) for v in got_back[12:]]
     qkv, hw, probs, attn, gx1, act, gpb, h2, gyp = kept
     gcols = 4 * gc + 2 * hid + 128
 

time: 306 us -> 292 us (0.954)
  Pallas kernels: 276 us -> 267 us
  local copies, waits for them, and re-layouts: 24 us -> 20.2 us
    pallas_call x1, Pallas kernels: 73 us -> 64.8 us  [shards(): pl.pallas_call(functools.partial(backward_kernel, steps=steps, **names),...]
    unnamed x13 -> x12, local copies, waits for them, and re-layouts: 15.4 us -> 14.6 us
where the time goes in v3:
time: 292 us; the launch traced here: 291 us
  Pallas kernels  267 us (91%)
  local copies, waits for them, and re-layouts  20.2 us (7%)
  other arithmetic  3.67 us (1%)
    pallas_call x1, Pallas kernels, reduce_all(): pl.pallas_call(functools.partial(reduce_kernel, n_dp=n_dp, n_mp=n_mp, tab...  99.6 us
    pallas_call x1, Pallas kernels, shards(): pl.pallas_call(functools.partial(backward_kernel, steps=steps, **names),...  64.8 us
    pallas_call x2, Pallas kernels, shards(): pl.pallas_call(functools.partial(forward_kernel, kept=len(kept), relayed=...  56.9 us
    pallas_call x1, Pallas kernels, gather_all(): pl.pallas_call(functools.partial(gather_kernel, n_dp=n_dp, n_mp=n_mp, wpo...  43.6 us
    unnamed x12, local copies, waits for them, and re-layouts  14.6 us

profile of v3, /device:TPU:0, one launch (start us, length us, event | category | flops | bytes accessed | tf_op | source)
XLA Modules:
  0.0 291.5 jit_solution(15836846611462684289)
XLA Ops:
  0.6 0.0 copy-start
  0.7 0.7 maximum_bitcast_fusion
  1.4 0.6 pad_convert_fusion.sm_ref
  2.0 0.8 copy.48
  2.7 0.8 copy.49
  3.5 0.0 copy-done
  3.5 1.6 concatenate.9.in_ref
  5.2 3.9 %constant_dynamic-slice_fusion = (bf16[6,196,512]{2,0,1:T(8,128)(2,1)S(1)}, bf16[6,196,512]{2,0,1:T(8,128)(2,1)S(1)}) fusion(bf16[24,196,512]{2,0,1:T(8,128)(2,1)} %param.19, s32[]{:T(128)S(6)} %select_n.4, bf16[24,196,512]{2,0,1:T(8,128)(2,1)} %param.18), kind=kLoop, calls=%fused_computation.4 | loop fusion | bytes 4816900 | tf_op jit(solution)/shard_map/dynamic_slice | solution.py:952
  9.1 1.4 copy.53.refs_1_
  10.5 1.4 copy.52.refs_0_
  11.9 43.6 %gather_weights.1 = (bf16[4,2,2,2,64,1664]{5,4,3,2,1,0:T(8,128)(2,1)}, f32[4,8,128]{2,1,0:T(8,128)}, f32[4,64,256]{2,1,0:T(8,128)}, f32[4,64,256]{2,1,0:T(8,128)}, s32[64,256]{1,0:T(8,128)}) custom-call(bf16[64,1664]{1,0:T(8,128)(2,1)} %concatenate.9.in_ref, f32[8,128]{1,0:T(8,128)} %pad_convert_fusion.sm_ref, s32[49,49]{1,0:T(8,128)} %rel_in.1, ...), custom_call_target="tpu_custom_call" | custom-call | tf_op jit(solution)/shard_map/gather_weights/pallas_call | solution.py:844
  55.5 18.4 %forward.2 = (bf16[1536,1536]{1,0:T(8,128)(2,1)}, bf16[1536,512]{1,0:T(8,128)(2,1)}, f32[24,4,64,256]{3,2,1,0:T(8,128)}, bf16[1248,512]{1,0:T(8,128)(2,1)}, bf16...) custom-call(bf16[6,196,512]{2,1,0:T(8,128)(2,1)} %copy.52.refs_0_, ...), custom_call_target="tpu_custom_call" | custom-call | tf_op jit(solution)/shard_map/forward/pallas_call | solution.py:985
  73.9 38.5 %forward.3 = (bf16[1536,1536]{1,0:T(8,128)(2,1)}, bf16[1536,512]{1,0:T(8,128)(2,1)}, f32[24,4,64,256]{3,2,1,0:T(8,128)}, bf16[1248,512]{1,0:T(8,128)(2,1)}, bf16...) custom-call(bf16[6,196,512]{2,1,0:T(8,128)(2,1)} %copy.52.refs_0_, ...), custom_call_target="tpu_custom_call", output_to_operand_aliasing={{0}: (10, {}), {1}: (11, {}), {2}: (12, {}), {3}: (13, {}),... | custom-call | tf_op jit(solution)/shard_map/forward/pallas_call | solution.py:985
  112.4 0.0 copy-start.2
  112.4 64.8 %backward.1 = (bf16[6,196,512]{2,1,0:T(8,128)(2,1)}, f32[4,64,256]{2,1,0:T(8,128)}, f32[8,512]{1,0:T(8,128)}, bf16[4,512,1664]{2,1,0:T(8,128)(2,1)}, bf16[4,2,2,196,512]{4,3,2,1,0:T(8,128)(2,1)}) custom-call(bf16[6,196,512]{2,1,0:T(8,128)(2,1)} %copy.52.refs_0_, f32[1248,512]{1,0:T(8,128)} %get-tuple-element.73.refs_1_.refs_10_, ...), custom_call_target="tpu_custom_call" | custom-call | tf_op jit(solution)/shard_map/backward/pallas_call | solution.py:1031
  177.2 0.0 copy-done.2
  177.3 2.4 pad_maximum_fusion
  179.6 4.0 %copy.50 = bf16[24,196,512]{2,0,1:T(8,128)(2,1)} copy(bf16[24,196,512]{2,1,0:T(8,128)(2,1)S(1)} %bitcast.28) | data formatting | bytes 9633792
  183.6 99.6 %reduce_gradients.1 = (f32[64,1664]{1,0:T(8,128)}, f32[16,256]{1,0:T(8,128)}, bf16[4,3,2,196,512]{4,3,2,1,0:T(8,128)(2,1)}) custom-call(bf16[4,2,2,2,64,1664]{5,4,3,2,1,0:T(8,128)(2,1)} %bitcast.29, s32[64,256]{1,0:T(8,128)} %get-tuple-element.87.rel_ref, f32[4,64,256]{2,1,0:T(8,128)} %get-tuple-element.88.tab_ref, f32[8,512]{1,0:T(8,128)} %get-tuple-element.89.qvs_ref, ...), custom_call_target="tpu_custom_call" | custom-call | tf_op jit(solution)/shard_map/reduce_gradients/pallas_call | solution.py:873
  283.2 0.0 copy-start.1
  283.2 6.3 %copy.51 = bf16[24,196,512]{2,0,1:T(8,128)(2,1)} copy(bf16[24,196,512]{2,1,0:T(8,128)(2,1)} %bitcast.30) | data formatting | bytes 9633792
  289.5 1.8 unpack.1
  291.3 0.0 copy-done.1
  (2 shorter events, 0.0 us)
Async XLA Ops:
  0.6 2.9 copy-start
  112.4 64.8 %copy-start.2 = (bf16[4,2,1,196,512]{4,3,2,1,0:T(8,128)(2,1)S(1)}, bf16[4,2,1,196,512]{4,3,2,1,0:T(8,128)(2,1)}, u32[]{:S(2)}) copy-start(bf16[4,2,1,196,512]{4,3,2,1,0:T(8,128)(2,1)} %get-tuple-element.72) | copy-start | bytes 4816900
  283.2 8.1 %copy-start.1 = (bf16[64,3,128]{2,0,1:T(8,128)(2,1)S(1)}, bf16[64,3,128]{2,0,1:T(8,128)(2,1)}, u32[]{:S(2)}) copy-start(bf16[64,3,128]{2,0,1:T(8,128)(2,1)} %param.22) | copy-start | bytes 147460
